TPU v7x, 768 devices: a whole 4x8x12 slice. The times are simulated.
768 devices in a mesh: inter: 192 (over y, z, core), intra: 4 (over x).
Axes of the slice: x: 4, y: 8, z: 12, core: 2. Of those that a mesh axis runs over, the one named last changes fastest.
Arguments:
- partials: bfloat16 [768, 192, 5120], P(('inter', 'intra')), may hold values from -24 to 24
- scales: bfloat16 [768, 192, 20], P(('inter', 'intra')), may hold values from 64 to 1024
- overflow_pos: int32 [768, 1], P(('inter', 'intra')), may hold values from -983040 to 983039, as said below
- weights: float32 [192, 5120], P('inter', 'intra'), may hold values from -6 to 6
- exponent: int32 [], replicated, may hold values from 10 to 16
Outputs:
- grad_out: float32 [192, 5120], P('inter', 'intra')
- block_scale: float32 [192, 20], P('inter', 'intra')
- master_out: float32 [192, 5120], P('inter', 'intra')
- new_exponent: int32 [], replicated
- overflow_count: int32 [], replicated
Inputs may be any that keep to these rules, and one draw needn't show every extreme that they name: `overflow_pos`: A negative entry means no overflow on that device; otherwise it is the flat position (row times 5120 plus column) of an overflowed value of that device's partial.
All inputs are finite; a program needn't handle non-finite values.
Results may differ from a plain program's by a relative error of at most 0.0005.
Values may be sent and summed in bfloat16 or wider, within the bound.
A program may use at most 64 MiB of HBM per device.

v0:
```python
import jax
import jax.numpy as jnp
from jax import lax
from jax.sharding import Mesh
from jax.sharding import PartitionSpec as P

INTER = ("inter_0", "inter_1", "inter_2")
INTER_INTRA = ("inter_0", "inter_1", "inter_2", "intra")


def in_one_piece(arrays, axis, split_dim, concat_dim, along):
    both = jnp.concatenate(arrays, axis=along)
    whole, at, gathered = (
        lax.all_to_all(both, axis, split_axis=split_dim, concat_axis=concat_dim, tiled=True),
        0,
        [],
    )
    for a in arrays:
        gathered.append(lax.slice_in_dim(whole, at, at + a.shape[along], axis=along))
        at += a.shape[along]
    return tuple(gathered)


def sum_in_order(pieces, axes, sequence):
    inside = pieces.shape[1:]
    pieces = pieces.reshape(*(lax.axis_size(a) for a in axes), *inside)
    pieces = jnp.moveaxis(pieces, sequence, range(len(axes))).reshape(-1, *inside)
    for k in sequence:
        pieces = lax.psum_scatter(pieces, axes[k], scatter_dimension=0, tiled=True)
    return pieces[0]


def in_blocks(shard, dim, size):
    lengths = shard.shape
    pieces = shard.reshape(*lengths[:dim], size, lengths[dim] // size, *lengths[dim + 1 :])
    return jnp.moveaxis(pieces, dim, 0)


def scatter_axes(shard, axes, sequence, dim):
    size = lax.axis_size(axes)
    return sum_in_order(in_blocks(shard, dim, size), axes, sequence)


def by_axis(shard, axes):
    for axis in axes:
        shard = lax.psum(shard, axis)
    return shard


def dequantize(levels, block_scales, block_len):
    dims_all = levels.shape
    expanded = levels.astype(jnp.float32).reshape(
        dims_all[0], dims_all[1], dims_all[2], block_scales.shape[3], block_len
    )
    expanded = expanded * block_scales.astype(jnp.float32)[..., None]
    return jnp.sum(expanded, axis=2).reshape(dims_all[0], dims_all[1], dims_all[3])


def on_device(partials, scales, overflow_pos, weights, exponent):
    inter_size = lax.axis_size(INTER)
    intra_size = lax.axis_size("intra")
    row_total = partials.shape[1]
    full_width = partials.shape[2]
    block_total = scales.shape[2]
    block_len = full_width // block_total
    share_rows = row_total // inter_size
    share_cols = full_width // intra_size
    share_blocks = block_total // intra_size
    local_flags = jnp.sum((overflow_pos >= 0).astype(jnp.float32))
    grouped = partials.reshape(inter_size, share_rows, intra_size, share_cols)
    grouped_scales = scales.reshape(inter_size, share_rows, intra_size, share_blocks)
    flag_copies = jnp.full((1, 1, intra_size, 1), local_flags, jnp.bfloat16)
    got_levels, got_scales, got_flags = (
        *in_one_piece((grouped, grouped_scales), "intra", 2, 2, 3),
        lax.all_to_all(flag_copies, "intra", split_axis=2, concat_axis=2, tiled=True),
    )
    group_sum = dequantize(got_levels, got_scales, block_len)
    group_flags = jnp.sum(got_flags.astype(jnp.float32))
    grad_sum = scatter_axes(group_sum, INTER, (2, 0, 1), 0)[0]
    flag_total = by_axis(group_flags, INTER)
    flag_count = flag_total.astype(jnp.int32)
    grad_out = grad_sum * jnp.exp2(-exponent.astype(jnp.float32))
    block_scale = (
        jnp.max(jnp.abs(grad_out.reshape(share_rows, share_blocks, block_len)), axis=2) / 127.0
    )
    master_out = jnp.where(flag_count == 0, weights - 0.5 * grad_out, weights)
    new_exponent = exponent - (flag_count > 0).astype(jnp.int32)
    return (grad_out, block_scale, master_out, new_exponent, flag_count)


def solution(mesh):
    torus = Mesh(
        mesh.devices.reshape(8, 12, 2, mesh.shape["intra"]),
        ("inter_0", "inter_1", "inter_2", "intra"),
    )
    return jax.shard_map(
        on_device,
        mesh=torus,
        in_specs=(
            P(INTER_INTRA, None, None),
            P(INTER_INTRA, None, None),
            P(INTER_INTRA, None),
            P(INTER, "intra"),
            P(),
        ),
        out_specs=(P(INTER, "intra"), P(INTER, "intra"), P(INTER, "intra"), P(), P()),
        check_vma=False,
    )
```

profile of v0, /device:TPU:1, one launch (start us, length us, event | category | flops | bytes accessed | tf_op | source)
XLA Modules:
  0.0 231.5 jit_solution(15461338316301885800)
XLA Ops:
  7.2 0.0 reduce-scatter.7.cloned.1.call-start
  7.2 0.7 reshape.91
  7.9 0.2 copy.19
  8.1 3.8 %reshape.90 = bf16[192,1,4,1280]{3,2,0,1:T(4,128)(2,1)S(1)} reshape(bf16[1,192,5120]{2,1,0:T(8,128)(2,1)} %param.5) | data formatting | bytes 3932160 | tf_op jit(solution)/shard_map/reshape | solution.py:70
  11.9 1.0 pad_maximum_fusion
  12.9 0.2 copy.20
  13.2 23.4 %all_to_all.10 = bf16[192,1,4,1285]{3,0,1,2:T(8,128)(2,1)S(1)} all-to-all(bf16[192,1,4,1285]{3,0,1,2:T(8,128)(2,1)S(1)} %copy.20), channel_id=1, replica_groups=mesh['inter_0'=8,'inter_1'=12,'inter_2'=2,'intra'=4] {'intra'}, dimensions={2} | all-to-all | bytes 3947520 | tf_op jit(solution)/shard_map/all_to_all | solution.py:14
  36.7 0.2 copy.22
  36.8 1.4 slice.8
  38.3 2.8 %copy.32 = bf16[192,1,4,1280]{0,3,2,1:T(8,128)(2,1)S(1)} copy(bf16[192,1,4,1280]{3,0,1,2:T(8,128)(2,1)} %slice.8) | data formatting | bytes 3932160
  41.1 0.4 mul.67
  41.5 1.9 multiply_reduce_fusion
  43.4 1.7 copy.23
  45.1 0.6 reshape_reshape_reshape.3
  45.7 1.0 copy.24
  46.8 0.0 copy-start
  46.8 1.0 copy.34
  47.8 0.0 reduce-scatter.7.cloned.1.call-update
  47.8 0.0 all-reduce.5.cloned.1.call-start
  47.9 34.9 %reduce-scatter.7.cloned.1.call-done = f32[96,1280]{1,0:T(8,128)} async-done(((f32[192,1280]{1,0:T(8,128)}), f32[96,1280]{1,0:T(8,128)}) %reduce-scatter.7.cloned.1.call-update) | async-done | bytes 491536
  82.7 2.1 reshape_bitcast_fusion
  84.9 0.0 all-reduce.5.cloned.1.call-update
  85.6 0.6 broadcast_in_dim.4
  86.1 3.2 %all-to-all-start.1 = ((bf16[1,1,4,1]{3,1,0,2:T(2,128)(2,1)}), bf16[1,1,4,1]{3,1,0,2:T(2,128)(2,1)S(1)}, u32[]{:S(2)}, u32[]{:S(2)}) async-start(bf16[1,1,4,1]{3,1,0,2:T(2,128)(2,1)} %broadcast_in_dim.4), calls=%async_computation.1 | async-start | bytes 4096 | tf_op jit(solution)/shard_map/all_to_all | solution.py:75
  90.1 1.3 dynamic-slice.2
  91.4 1.3 dynamic-slice
  92.7 0.7 all-to-all-done.1
  93.4 0.6 convert_reduce_fusion
  94.6 13.3 %psum.21 = f32[]{:T(128)} all-reduce(f32[]{:T(128)} %convert_reduce_fusion), channel_id=1, replica_groups=mesh['inter_0'=8,'inter_1'=12,'inter_2'=2,'intra'=4] {'inter_0'}, use_global_device_ids=true, to_apply=%region_6.0 | all-reduce | flops 1 | bytes 8 | tf_op jit(solution)/shard_map/psum | solution.py:46
  108.0 56.5 %all-reduce.5.cloned.1.call-done = f32[96,1,1,1280]{3,2,0,1:T(1,128)} async-done(((f32[96,1,1,1280]{3,2,0,1:T(1,128)}), f32[96,1,1,1280]{3,2,0,1:T(1,128)}) %all-reduce.5.cloned.1.call-update) | async-done | bytes 491536
  164.5 0.8 constant_dynamic-slice_fusion
  165.3 34.4 %all-reduce.2 = (f32[12,1,1,1280]{3,2,0,1:T(1,128)S(1)}, f32[]{:T(128)}) all-reduce(f32[12,1,1,1280]{3,2,0,1:T(1,128)S(1)} %constant_dynamic-slice_fusion, f32[]{:T(128)} %psum.21), channel_id=4, replica_groups=mesh['inter_0'=8,'inter_1'=12,'inter_2'=2,'intra'=4] {'inter_1'}, use_global_device_ids=true, to_apply=%region_3.0.clone | all-reduce | flops 15361 | bytes 122888
  199.7 19.4 %psum.23 = f32[]{:T(128)} all-reduce(f32[]{:T(128)} %get-tuple-element.6), channel_id=1, replica_groups=mesh['inter_0'=8,'inter_1'=12,'inter_2'=2,'intra'=4] {'inter_2'}, use_global_device_ids=true, to_apply=%region_8.0 | all-reduce | flops 1 | bytes 8 | tf_op jit(solution)/shard_map/psum | solution.py:46
  219.8 0.7 abs_reduce_fusion
  220.5 0.1 reduce_max.9
  220.6 0.5 multiply_bitcast_fusion
  221.1 0.0 copy-done
  221.1 1.3 broadcast_select_fusion
  (2 shorter events, 0.0 us)
Async XLA Ops:
  7.2 75.6 %reduce-scatter.7.cloned.1.call-start = ((), (), s32[]{:S(2)}) async-start(), calls=%async_computation.3 | async-start | bytes 1474560
  46.8 174.4 %copy-start = (f32[1,1280]{1,0:T(1,128)S(1)}, f32[1,1280]{1,0:T(1,128)}, u32[]{:S(2)}) copy-start(f32[1,1280]{1,0:T(1,128)} %param.8) | copy-start | bytes 15364
  47.8 116.7 %all-reduce.5.cloned.1.call-start = ((), (), s32[]{:S(2)}) async-start(), calls=%async_computation.4 | async-start | bytes 983040
  86.1 7.3 %all-to-all-start.1 = ((bf16[1,1,4,1]{3,1,0,2:T(2,128)(2,1)}), bf16[1,1,4,1]{3,1,0,2:T(2,128)(2,1)S(1)}, u32[]{:S(2)}, u32[]{:S(2)}) async-start(bf16[1,1,4,1]{3,1,0,2:T(2,128)(2,1)} %broadcast_in_dim.4), calls=%async_computation.1 | async-start | bytes 4096 | tf_op jit(solution)/shard_map/all_to_all | solution.py:75
Sparse Core Ops, SparseCore 0:
  47.9 34.7 reduce-scatter.6
  85.1 79.3 all-reduce.4
where the time goes:
time: 232 us
  waiting for transfers between devices  92.2 us (40%)
  blocking collectives  90.5 us (39%)
  local copies, waits for them, and re-layouts  20.3 us (9%)
  between operations  19.1 us (8%)
  other arithmetic  6.2 us (3%)
  starting transfers between devices  3.3 us (1%)
    unnamed x4, waiting for transfers between devices  91.4 us
    unnamed x1, blocking collectives  34.4 us
    psum x2, blocking collectives, by_axis(): shard = lax.psum(shard, axis)  32.7 us
    all_to_all x1, blocking collectives, in_one_piece(): lax.all_to_all(both, axis, split_axis=split_dim, concat_axis=concat_dim,...  23.4 us
    unnamed x8, local copies, waits for them, and re-layouts  9.44 us
  transfers between devices with their start and end apart: 3, of which 3 were waited for; matrix products, arithmetic and copies ran while one was open for 2% of the time, Pallas kernels for 0%

commit v1 on v0

v1 whole, which is shorter than its diff:
```python
import functools

import jax
import jax.numpy as jnp
from jax import lax
from jax.experimental import pallas as pl
from jax.experimental.pallas import tpu as pltpu
from jax.sharding import PartitionSpec as P

MESH = pl.DeviceIdType.MESH
NX, NY, NZ = 4, 8, 12
ZC = 2 * NZ
TI, TJ = ZC // 8, 5
HALF = TJ * 128
TOP = 32767.0


def wait(ref, sem):
    pltpu.make_async_copy(ref, ref, sem).wait()


def far_first(k, n):
    m = (k + 1) // 2
    return jnp.where(k % 2 == 1, n // 2 - m, n // 2 + m)


def encode(tiles, out):
    lane = lax.broadcasted_iota(jnp.int32, (8, 128), 1)
    tops = jnp.zeros((8, 128), jnp.float32)
    flat = []
    for row in tiles:
        peak = functools.reduce(jnp.maximum, [jnp.abs(t) for t in row])
        peak = jnp.maximum(jnp.max(peak, axis=1, keepdims=True), 1e-30)
        top = jnp.ceil(jnp.log2(jnp.broadcast_to(peak, (8, 128))) + 1e-3)
        tops = jnp.where(lane == len(flat) // TJ, top, tops)
        factor = jnp.exp2(-top) * TOP
        flat += [t * factor for t in row]
    flat.append(tops)
    for p in range(len(flat) // 2):
        pair = jnp.concatenate([flat[2 * p], flat[2 * p + 1]], axis=0)
        out[p] = jnp.round(pair).astype(jnp.int32).astype(jnp.int16)


def decode(ref):
    flat = []
    for p in range((TI * TJ + 1) // 2):
        pair = ref[p].astype(jnp.int32).astype(jnp.float32)
        flat += [pair[:8], pair[8:]]
    factors = jnp.exp2(flat[TI * TJ]) * (1.0 / TOP)
    return [
        [flat[i * TJ + j] * jnp.broadcast_to(factors[:, i : i + 1], (8, 128)) for j in range(TJ)]
        for i in range(TI)
    ]


def add(a, b):
    return [[p + q for p, q in zip(r, s)] for r, s in zip(a, b)]


def kernel(
    part, scales, pos, weights, exponent,
    grad, block_scale, master, new_exponent, count,
    lev, par, sc, sco, xs, xr, xo, ys, yr, zs, zr, fs, fx, fy,
    load_sem, sc_sem, core_send, core_recv, x_send, x_recv, y_send, y_recv, z_send, z_recv,
    fx_send, fx_recv, fy_send, fy_recv,
):
    inter, x = lax.axis_index("inter"), lax.axis_index("intra")
    c, zc = inter % 2, inter % ZC
    z, y = zc // 2, inter // ZC
    partner = inter + 1 - 2 * c

    for h, side in ((1, 1 - c), (0, c)):
        for xt in range(NX):
            columns = pl.ds(pl.multiple_of(xt * 2 * HALF + side * HALF, 128), HALF)
            pltpu.make_async_copy(part.at[:, :, :, columns], lev.at[h, :, xt], load_sem.at[h]).start()
    pltpu.make_async_copy(scales, sc.at[0], sc_sem.at[0]).start()

    barrier = pltpu.get_barrier_semaphore()

    def meet(to):
        pl.semaphore_signal(barrier, inc=1, device_id=to, device_id_type=MESH)

    for d in range(1, NX):
        meet((inter, (x + d) % NX))
    for d in range(1, NY):
        meet(((y + d) % NY * ZC + zc, x))
    for d in range(1, ZC):
        meet((y * ZC + (zc + d) % ZC, x))
    fs[0] = jnp.full((1, 128), (pos[0, 0] >= 0).astype(jnp.float32), jnp.float32)
    wait(sc.at[0], sc_sem.at[0])
    wait(lev.at[1], load_sem.at[1])
    pl.semaphore_wait(barrier, NX - 1 + NY - 1 + ZC - 1)

    def core_copy(k):
        yt = (y + far_first(k, NY)) % NY
        return pltpu.make_async_remote_copy(
            lev.at[1, yt], par.at[yt], core_send.at[k], core_recv.at[k], (partner, x), MESH
        )

    scale_copy = pltpu.make_async_remote_copy(
        sc.at[0], sc.at[1], sc_sem.at[1], sc_sem.at[2], (partner, x), MESH
    )
    scale_copy.start()

    @pl.loop(0, NY)
    def _(k):
        core_copy(k).start()

    def flag_x(d):
        return pltpu.make_async_remote_copy(
            fs.at[0], fx.at[d - 1], fx_send.at[d - 1], fx_recv.at[d - 1], (inter, (x + d) % NX), MESH
        )

    for d in range(1, NX):
        flag_x(d).start()
    wait(lev.at[0], load_sem.at[0])
    scale_copy.wait()

    def widen(h):
        @pl.loop(0, NY)
        def _(g):
            for i in range(TI):
                sco[h, g, i, :, 0:20] = sc[h, g, i].astype(jnp.float32)

    widen(0)
    widen(1)

    def x_copy(k, d):
        return pltpu.make_async_remote_copy(
            xs.at[k, d - 1], xr.at[k, d - 1], x_send, x_recv.at[k], (inter, (x + d) % NX), MESH
        )

    @pl.loop(0, NY)
    def _(k):
        yt = (y + far_first(k, NY)) % NY
        wait(par.at[yt], core_recv.at[k])
        for d in (2, 1, 3, 0):
            xt = (x + d) % NX
            shift = (128 - (xt * TJ + 2 * c)) % 128
            tiles = []
            for i in range(TI):
                total = None
                for h in range(2):
                    s = pltpu.roll(sco[h, yt, i], shift, 1)
                    b = [jnp.broadcast_to(s[:, n : n + 1], (8, 128)) for n in range(3)]
                    even = c == 0
                    b = [b[0], jnp.where(even, b[0], b[1]), b[1], jnp.where(even, b[1], b[2]), b[2]]
                    levels = lev[0, yt, xt, i] if h == 0 else par[yt, xt, i]
                    levels = levels.astype(jnp.float32)
                    term = [levels[:, j * 128 : (j + 1) * 128] * b[j] for j in range(TJ)]
                    total = term if total is None else [p + q for p, q in zip(total, term)]
                tiles.append(total)
            if d:
                encode(tiles, xs.at[k, d - 1])
                x_copy(k, d).start()
            else:
                for i in range(TI):
                    for j in range(TJ):
                        xo[k, i * TJ + j] = tiles[i][j]

    flags = fs[0]
    for d in range(1, NX):
        wait(fx.at[d - 1], fx_recv.at[d - 1])
        flags = flags + fx[d - 1]
    fs[1] = flags

    def flag_y(d):
        return pltpu.make_async_remote_copy(
            fs.at[1], fy.at[d - 1], fy_send.at[d - 1], fy_recv.at[d - 1], ((y + d) % NY * ZC + zc, x), MESH
        )

    for d in range(1, NY):
        flag_y(d).start()

    def y_copy(k):
        return pltpu.make_async_remote_copy(
            ys.at[k], yr.at[k], y_send.at[k], y_recv.at[k], ((y + far_first(k, NY)) % NY * ZC + zc, x), MESH
        )

    def x_sum(k):
        wait(xr.at[k], x_recv.at[k])
        tiles = [[xo[k, i * TJ + j] for j in range(TJ)] for i in range(TI)]
        for d in range(1, NX):
            tiles = add(tiles, decode(xr.at[k, d - 1]))
        return tiles

    @pl.loop(0, NY - 1)
    def _(k):
        encode(x_sum(k), ys.at[k])
        y_copy(k).start()

    tiles = x_sum(NY - 1)
    for d in range(1, NY):
        wait(fy.at[d - 1], fy_recv.at[d - 1])
        flags = flags + fy[d - 1]
    for k in range(NY - 1):
        wait(yr.at[k], y_recv.at[k])
        tiles = add(tiles, decode(yr.at[k]))
    for i in range(TI):
        for j in range(TJ):
            zs[pl.ds(i * 64 + j, 8, stride=8), :] = tiles[i][j]
        zs[pl.ds(i * 64 + TJ, 8, stride=8), :] = jnp.broadcast_to(flags, (8, 128))

    def rows(n):
        return pl.ds(pl.multiple_of(n * 8, 8), TJ + 1)

    def z_copy(k):
        to = (zc + far_first(k, ZC)) % ZC
        return pltpu.make_async_remote_copy(
            zs.at[rows(to)], zr.at[rows(zc)], z_send.at[k], z_recv.at[k], (y * ZC + to, x), MESH
        )

    @pl.loop(0, ZC - 1)
    def _(k):
        z_copy(k).start()

    own = pl.ds(pl.multiple_of(zc * 8, 8), 8)
    mine = zs[own, :]

    for d in range(1, NX):
        wait(fs.at[0], fx_send.at[d - 1])
    for d in range(1, NY):
        wait(fs.at[1], fy_send.at[d - 1])
    wait(xs, x_send)

    @pl.loop(0, NY)
    def _(k):
        wait(lev.at[1, k], core_send.at[k])

    @pl.loop(0, NY - 1)
    def _(k):
        wait(ys.at[k], y_send.at[k])

    @pl.loop(0, ZC - 1)
    def _(k):
        wait(zr.at[rows(k)], z_recv.at[k])

    zr[own, :] = mine
    halves = [
        functools.reduce(jnp.add, [zr[(2 * n + h) * 8 : (2 * n + h) * 8 + 8, :] for n in range(NZ)])
        for h in range(2)
    ]
    total = halves[0][TJ, 0] + halves[1][TJ, 0]
    flagged = total.astype(jnp.int32)
    factor = jnp.exp2(jnp.full((8, 128), -exponent[0].astype(jnp.float32), jnp.float32))
    peaks = []
    for h in range(2):
        g = halves[h] * factor
        peak = jnp.max(jnp.abs(g), axis=1, keepdims=True)
        for j in range(TJ):
            at = slice((h * TJ + j) * 128, (h * TJ + j + 1) * 128)
            w = weights[:, at]
            grad[:, at] = g[j : j + 1]
            master[:, at] = jnp.where(flagged == 0, w - 0.5 * g[j : j + 1], w)
            peaks.append(peak[j : j + 1])
    lane = lax.broadcasted_iota(jnp.int32, (1, 128), 1)
    scale = jnp.zeros((1, 128), jnp.float32)
    for b in range(TJ):
        top = jnp.maximum(peaks[2 * b], peaks[2 * b + 1]) / 127.0
        scale = jnp.where(lane == b, jnp.broadcast_to(top, (1, 128)), scale)
    block_scale[...] = scale[:, :TJ]
    new_exponent[0] = exponent[0] - (flagged > 0).astype(jnp.int32)
    count[0] = flagged

    @pl.loop(0, ZC - 1)
    def _(k):
        wait(zr.at[rows(k)], z_send.at[k])


def on_device(partials, scales, overflow_pos, weights, exponent):
    vmem, smem, anywhere = (
        pl.BlockSpec(memory_space=m) for m in (pltpu.VMEM, pltpu.SMEM, pl.ANY)
    )
    f32, i16, dma = jnp.float32, jnp.int16, pltpu.SemaphoreType.DMA
    code = (8, 16, 128)
    grad, block_scale, master, new_exponent, count = pl.pallas_call(
        kernel,
        out_shape=(
            jax.ShapeDtypeStruct((1, 2 * HALF), f32),
            jax.ShapeDtypeStruct((1, TJ), f32),
            jax.ShapeDtypeStruct((1, 2 * HALF), f32),
            jax.ShapeDtypeStruct((1,), jnp.int32),
            jax.ShapeDtypeStruct((1,), jnp.int32),
        ),
        in_specs=[anywhere, anywhere, smem, vmem, smem],
        out_specs=[vmem, vmem, vmem, smem, smem],
        scratch_shapes=[
            pltpu.VMEM((2, NY, NX, TI, 8, HALF), jnp.bfloat16),
            pltpu.VMEM((NY, NX, TI, 8, HALF), jnp.bfloat16),
            pltpu.VMEM((2, NY, TI, 8, 20), jnp.bfloat16),
            pltpu.VMEM((2, NY, TI, 8, 128), f32),
            pltpu.VMEM((NY, NX - 1, *code), i16),
            pltpu.VMEM((NY, NX - 1, *code), i16),
            pltpu.VMEM((NY, TI * TJ, 8, 128), f32),
            pltpu.VMEM((NY - 1, *code), i16),
            pltpu.VMEM((NY - 1, *code), i16),
            pltpu.VMEM((ZC * 8, 128), f32),
            pltpu.VMEM((ZC * 8, 128), f32),
            pltpu.VMEM((2, 1, 128), f32),
            pltpu.VMEM((NX - 1, 1, 128), f32),
            pltpu.VMEM((NY - 1, 1, 128), f32),
            dma((2,)), dma((3,)), dma((NY,)), dma((NY,)), dma, dma((NY,)),
            dma((NY - 1,)), dma((NY - 1,)), dma((ZC - 1,)), dma((ZC - 1,)),
            dma((NX - 1,)), dma((NX - 1,)), dma((NY - 1,)), dma((NY - 1,)),
        ],
        compiler_params=pltpu.CompilerParams(collective_id=0, has_side_effects=True),
    )(
        partials.reshape(NY, TI, 8, partials.shape[2]),
        scales.reshape(NY, TI, 8, scales.shape[2]),
        overflow_pos,
        weights,
        exponent.reshape(1),
    )
    return grad, block_scale, master, new_exponent.reshape(()), count.reshape(())


def solution(mesh):
    return jax.shard_map(
        on_device,
        mesh=mesh,
        in_specs=(
            P(("inter", "intra"), None, None),
            P(("inter", "intra"), None, None),
            P(("inter", "intra"), None),
            P("inter", "intra"),
            P(),
        ),
        out_specs=(P("inter", "intra"), P("inter", "intra"), P("inter", "intra"), P(), P()),
        check_vma=False,
    )
```

time: 232 us -> 56.5 us (0.24)
  waiting for transfers between devices: 92.2 us -> 0 us
  blocking collectives: 90.5 us -> 0 us
  Pallas kernels: 0 us -> 45.5 us
  local copies, waits for them, and re-layouts: 20.3 us -> 5.11 us
  between operations: 19.1 us -> 5.44 us
  other arithmetic: 6.2 us -> 0 us
  starting transfers between devices: 3.3 us -> 0 us
    unnamed x4 -> x0, waiting for transfers between devices: 91.4 us -> none
    pallas_call x0 -> x1, Pallas kernels: none -> 45.5 us  [on_device(): pl.pallas_call(kernel, out_shape=(jax.ShapeDtypeStruct((1, 2 * HALF), f32...]
    unnamed x1 -> x0, blocking collectives: 34.4 us -> none
    psum x2 -> x0, blocking collectives: 32.7 us -> none  [by_axis(): shard = lax.psum(shard, axis)]
    all_to_all x1 -> x0, blocking collectives: 23.4 us -> none  [in_one_piece(): lax.all_to_all(both, axis, split_axis=split_dim, concat_axis=concat_dim,...]
    reshape x3 -> x0, local copies, waits for them, and re-layouts: 4.69 us -> none  [the longest x1 3.76 us: on_device(): grouped = partials.reshape(inter_size, share_rows, intra_size, share_cols)]
    unnamed x8 -> x4, local copies, waits for them, and re-layouts: 9.44 us -> 5.11 us
    all_to_all x1 -> x0, starting transfers between devices: 3.22 us -> none  [on_device(): lax.all_to_all(flag_copies, 'intra', split_axis=2, concat_axis=2, tiled=T...]
  transfers between devices with their start and end apart: 3 -> 0, of which waited for: 3 -> 0; matrix products, arithmetic and copies ran while one was open for 2% -> 0% of each run, Pallas kernels for 0% -> 0%
where the time goes in v1:
time: 56.5 us; the launch traced here: 56.1 us
  Pallas kernels  45.5 us (81%)
  between operations  5.44 us (10%)
  local copies, waits for them, and re-layouts  5.11 us (9%)
    pallas_call x1, Pallas kernels, on_device(): pl.pallas_call(kernel, out_shape=(jax.ShapeDtypeStruct((1, 2 * HALF), f32...  45.5 us
    unnamed x4, local copies, waits for them, and re-layouts  5.11 us

profile of v1, /device:TPU:1, one launch (start us, length us, event | category | flops | bytes accessed | tf_op | source)
XLA Modules:
  0.0 56.1 jit_solution(10419565486132912316)
XLA Ops:
  1.9 1.4 %copy.10 = bf16[1,192,20]{2,1,0:T(8,128)(2,1)} copy(bf16[1,192,20]{1,2,0:T(8,128)(2,1)} %param.6) | data formatting | bytes 15360 | tf_op args[1]
  3.4 45.5 %shard_map.92 = (f32[1,1280]{1,0:T(1,128)}, f32[1,5]{1,0:T(1,128)}, f32[1,1280]{1,0:T(1,128)}, s32[1]{0:T(128)}, s32[1]{0:T(128)}) custom-call(bf16[8,3,8,5120]{3,2,1,0:T(8,128)(2,1)} %bitcast.6, bf16[8,3,8,20]{3,2,1,0:T(8,128)(2,1)} %bitcast.7, s32[1,1]{1,0:T(1,128)S(6)} %copy.16.pos, f32[1,1280]{1,0:T(1,128)} %weights.1, s32[1]{0:T(128)} %bitcast.5.exponent), custom_call_target="tpu_custom_call" | custom-call | tf_op jit(solution)/shard_map/pallas_call | solution.py:276
  48.9 1.3 %copy.18 = f32[1,1280]{1,0:T(1,128)} copy(f32[1,1280]{1,0:T(1,128)} %get-tuple-element.20) | data formatting | bytes 10240
  50.2 1.1 %copy.19 = f32[1,5]{1,0:T(1,128)} copy(f32[1,5]{1,0:T(1,128)} %get-tuple-element.21) | data formatting | bytes 40
  51.3 1.3 %copy.20 = f32[1,1280]{1,0:T(1,128)} copy(f32[1,1280]{1,0:T(1,128)} %get-tuple-element.22) | data formatting | bytes 10240

commit v2 on v1

--- a/solution.py
+++ b/solution.py
@@ -58,10 +58,10 @@
 
 
 def kernel(
-    part, scales, pos, weights, exponent,
-    grad, block_scale, master, new_exponent, count,
-    lev, par, sc, sco, xs, xr, xo, ys, yr, zs, zr, fs, fx, fy,
-    load_sem, sc_sem, core_send, core_recv, x_send, x_recv, y_send, y_recv, z_send, z_recv,
+    part, scales, pos, exponent,
+    out,
+    lev, par, sc, st, sco, flag, power, xs, xr, xo, ys, yr, zs, zr, fs, fx, fy,
+    load_sem, sc_sem, flag_sem, power_sem, near, core_send, core_recv, x_send, x_recv, y_send, y_recv, z_send, z_recv,
     fx_send, fx_recv, fy_send, fy_recv,
 ):
     inter, x = lax.axis_index("inter"), lax.axis_index("intra")
@@ -75,21 +75,38 @@
             pltpu.make_async_copy(part.at[:, :, :, columns], lev.at[h, :, xt], load_sem.at[h]).start()
     pltpu.make_async_copy(scales, sc.at[0], sc_sem.at[0]).start()
 
+    pltpu.make_async_copy(pos, flag, flag_sem).start()
+    pltpu.make_async_copy(exponent, power, power_sem).start()
+
     barrier = pltpu.get_barrier_semaphore()
 
-    def meet(to):
-        pl.semaphore_signal(barrier, inc=1, device_id=to, device_id_type=MESH)
-
+    def along_y(d):
+        return ((y + d) % NY * ZC + zc, x)
+
+    def along_z(d):
+        return (y * ZC + (zc + 2 * d) % ZC, x)
+
+    def tell(sem, to):
+        pl.semaphore_signal(sem, inc=1, device_id=to, device_id_type=MESH)
+
+    def tell_both(sem, along, n, d):
+        tell(near.at[sem], along(d))
+        tell(near.at[sem], along(n - d))
+
+    tell(barrier, (partner, x))
     for d in range(1, NX):
-        meet((inter, (x + d) % NX))
-    for d in range(1, NY):
-        meet(((y + d) % NY * ZC + zc, x))
-    for d in range(1, ZC):
-        meet((y * ZC + (zc + d) % ZC, x))
-    fs[0] = jnp.full((1, 128), (pos[0, 0] >= 0).astype(jnp.float32), jnp.float32)
-    wait(sc.at[0], sc_sem.at[0])
-    wait(lev.at[1], load_sem.at[1])
-    pl.semaphore_wait(barrier, NX - 1 + NY - 1 + ZC - 1)
+        tell(barrier, (inter, (x + d) % NX))
+    for d in (1, NY - 1):
+        tell(barrier, along_y(d))
+    for d in (1, NZ - 1):
+        tell(barrier, along_z(d))
+    with jax.named_scope("load"):
+        wait(sc.at[0], sc_sem.at[0])
+        wait(lev.at[1], load_sem.at[1])
+    with jax.named_scope("barrier"):
+        pl.semaphore_wait(barrier, 1 + NX - 1 + 2 + 2)
+    tell_both(0, along_y, NY, 1)
+    tell_both(1, along_z, NZ, 1)
 
     def core_copy(k):
         yt = (y + far_first(k, NY)) % NY
@@ -111,19 +128,21 @@
             fs.at[0], fx.at[d - 1], fx_send.at[d - 1], fx_recv.at[d - 1], (inter, (x + d) % NX), MESH
         )
 
+    wait(flag, flag_sem)
+    wait(power, power_sem)
+    fs[0] = jnp.full((1, 128), (flag[0, 0] >= 0).astype(jnp.float32), jnp.float32)
     for d in range(1, NX):
         flag_x(d).start()
-    wait(lev.at[0], load_sem.at[0])
-    scale_copy.wait()
-
-    def widen(h):
-        @pl.loop(0, NY)
-        def _(g):
-            for i in range(TI):
-                sco[h, g, i, :, 0:20] = sc[h, g, i].astype(jnp.float32)
-
-    widen(0)
-    widen(1)
+    with jax.named_scope("wait_scale"):
+        wait(lev.at[0], load_sem.at[0])
+        scale_copy.wait()
+
+    with jax.named_scope("scales"):
+        for h in range(2):
+            st[h, :20, : NY * ZC] = sc[h].astype(jnp.float32)
+            for r in range(0, NY * ZC, 128):
+                n = min(128, NY * ZC - r) // 8
+                sco[h, r // 8 : r // 8 + n, :, :32] = st[h, :, r : r + 128].T.reshape(16, 8, 32)[:n]
 
     def x_copy(k, d):
         return pltpu.make_async_remote_copy(
@@ -133,7 +152,8 @@
     @pl.loop(0, NY)
     def _(k):
         yt = (y + far_first(k, NY)) % NY
-        wait(par.at[yt], core_recv.at[k])
+        with jax.named_scope("wait_core"):
+            wait(par.at[yt], core_recv.at[k])
         for d in (2, 1, 3, 0):
             xt = (x + d) % NX
             shift = (128 - (xt * TJ + 2 * c)) % 128
@@ -141,7 +161,7 @@
             for i in range(TI):
                 total = None
                 for h in range(2):
-                    s = pltpu.roll(sco[h, yt, i], shift, 1)
+                    s = pltpu.roll(sco[h, yt * TI + i], shift, 1)
                     b = [jnp.broadcast_to(s[:, n : n + 1], (8, 128)) for n in range(3)]
                     even = c == 0
                     b = [b[0], jnp.where(even, b[0], b[1]), b[1], jnp.where(even, b[1], b[2]), b[2]]
@@ -158,15 +178,24 @@
                     for j in range(TJ):
                         xo[k, i * TJ + j] = tiles[i][j]
 
+    pl.semaphore_wait(near.at[0], 2)
+    pl.semaphore_wait(near.at[1], 2)
+    tell_both(2, along_y, NY, 2)
+    tell_both(3, along_z, NZ, 2)
+
     flags = fs[0]
     for d in range(1, NX):
         wait(fx.at[d - 1], fx_recv.at[d - 1])
         flags = flags + fx[d - 1]
     fs[1] = flags
+    with jax.named_scope("near"):
+        pl.semaphore_wait(near.at[2], 2)
+        pl.semaphore_wait(near.at[3], 2)
+    tell_both(4, along_z, NZ, 4)
 
     def flag_y(d):
         return pltpu.make_async_remote_copy(
-            fs.at[1], fy.at[d - 1], fy_send.at[d - 1], fy_recv.at[d - 1], ((y + d) % NY * ZC + zc, x), MESH
+            fs.at[1], fy.at[d - 1], fy_send.at[d - 1], fy_recv.at[d - 1], along_y(d), MESH
         )
 
     for d in range(1, NY):
@@ -174,11 +203,12 @@
 
     def y_copy(k):
         return pltpu.make_async_remote_copy(
-            ys.at[k], yr.at[k], y_send.at[k], y_recv.at[k], ((y + far_first(k, NY)) % NY * ZC + zc, x), MESH
+            ys.at[k], yr.at[k], y_send.at[k], y_recv.at[k], along_y(far_first(k, NY)), MESH
         )
 
     def x_sum(k):
-        wait(xr.at[k], x_recv.at[k])
+        with jax.named_scope("wait_x"):
+            wait(xr.at[k], x_recv.at[k])
         tiles = [[xo[k, i * TJ + j] for j in range(TJ)] for i in range(TI)]
         for d in range(1, NX):
             tiles = add(tiles, decode(xr.at[k, d - 1]))
@@ -194,7 +224,8 @@
         wait(fy.at[d - 1], fy_recv.at[d - 1])
         flags = flags + fy[d - 1]
     for k in range(NY - 1):
-        wait(yr.at[k], y_recv.at[k])
+        with jax.named_scope("wait_y"):
+            wait(yr.at[k], y_recv.at[k])
         tiles = add(tiles, decode(yr.at[k]))
     for i in range(TI):
         for j in range(TJ):
@@ -210,6 +241,8 @@
             zs.at[rows(to)], zr.at[rows(zc)], z_send.at[k], z_recv.at[k], (y * ZC + to, x), MESH
         )
 
+    pl.semaphore_wait(near.at[4], 2)
+
     @pl.loop(0, ZC - 1)
     def _(k):
         z_copy(k).start()
@@ -231,21 +264,31 @@
     def _(k):
         wait(ys.at[k], y_send.at[k])
 
+    with jax.named_scope("wait_z"):
+
+        @pl.loop(0, ZC - 1)
+        def _(k):
+            wait(zr.at[rows(k)], z_recv.at[k])
+
+    zr[own, :] = mine
+    for h in range(2):
+        out[h * 8 : h * 8 + 8, :] = functools.reduce(
+            jnp.add, [zr[(2 * n + h) * 8 : (2 * n + h) * 8 + 8, :] for n in range(NZ)]
+        )
+    out[7:8, :] = jnp.full((1, 128), power[0].astype(jnp.float32), jnp.float32)
+
     @pl.loop(0, ZC - 1)
     def _(k):
-        wait(zr.at[rows(k)], z_recv.at[k])
-
-    zr[own, :] = mine
-    halves = [
-        functools.reduce(jnp.add, [zr[(2 * n + h) * 8 : (2 * n + h) * 8 + 8, :] for n in range(NZ)])
-        for h in range(2)
-    ]
-    total = halves[0][TJ, 0] + halves[1][TJ, 0]
+        wait(zr.at[rows(k)], z_send.at[k])
+
+
+def finish(sums, weights, grad, block_scale, master, new_exponent, count):
+    total = sums[TJ, 0] + sums[8 + TJ, 0]
     flagged = total.astype(jnp.int32)
-    factor = jnp.exp2(jnp.full((8, 128), -exponent[0].astype(jnp.float32), jnp.float32))
+    factor = jnp.exp2(-jnp.broadcast_to(sums[7:8, :], (8, 128)))
     peaks = []
     for h in range(2):
-        g = halves[h] * factor
+        g = sums[h * 8 : h * 8 + 8, :] * factor
         peak = jnp.max(jnp.abs(g), axis=1, keepdims=True)
         for j in range(TJ):
             at = slice((h * TJ + j) * 128, (h * TJ + j + 1) * 128)
@@ -259,36 +302,29 @@
         top = jnp.maximum(peaks[2 * b], peaks[2 * b + 1]) / 127.0
         scale = jnp.where(lane == b, jnp.broadcast_to(top, (1, 128)), scale)
     block_scale[...] = scale[:, :TJ]
-    new_exponent[0] = exponent[0] - (flagged > 0).astype(jnp.int32)
+    new_exponent[0] = sums[7, 0].astype(jnp.int32) - (flagged > 0).astype(jnp.int32)
     count[0] = flagged
 
-    @pl.loop(0, ZC - 1)
-    def _(k):
-        wait(zr.at[rows(k)], z_send.at[k])
-
 
 def on_device(partials, scales, overflow_pos, weights, exponent):
-    vmem, smem, anywhere = (
-        pl.BlockSpec(memory_space=m) for m in (pltpu.VMEM, pltpu.SMEM, pl.ANY)
+    vmem, smem, hbm = (
+        pl.BlockSpec(memory_space=m) for m in (pltpu.VMEM, pltpu.SMEM, pltpu.HBM)
     )
     f32, i16, dma = jnp.float32, jnp.int16, pltpu.SemaphoreType.DMA
     code = (8, 16, 128)
-    grad, block_scale, master, new_exponent, count = pl.pallas_call(
+    sums = pl.pallas_call(
         kernel,
-        out_shape=(
-            jax.ShapeDtypeStruct((1, 2 * HALF), f32),
-            jax.ShapeDtypeStruct((1, TJ), f32),
-            jax.ShapeDtypeStruct((1, 2 * HALF), f32),
-            jax.ShapeDtypeStruct((1,), jnp.int32),
-            jax.ShapeDtypeStruct((1,), jnp.int32),
-        ),
-        in_specs=[anywhere, anywhere, smem, vmem, smem],
-        out_specs=[vmem, vmem, vmem, smem, smem],
+        out_shape=jax.ShapeDtypeStruct((16, 128), f32),
+        in_specs=[hbm] * 4,
+        out_specs=vmem,
         scratch_shapes=[
             pltpu.VMEM((2, NY, NX, TI, 8, HALF), jnp.bfloat16),
             pltpu.VMEM((NY, NX, TI, 8, HALF), jnp.bfloat16),
-            pltpu.VMEM((2, NY, TI, 8, 20), jnp.bfloat16),
-            pltpu.VMEM((2, NY, TI, 8, 128), f32),
+            pltpu.VMEM((2, 20, NY * ZC), jnp.bfloat16),
+            pltpu.VMEM((2, 32, 256), f32),
+            pltpu.VMEM((2, NY * TI, 8, 128), f32),
+            pltpu.SMEM((1, 1), jnp.int32),
+            pltpu.SMEM((1,), jnp.int32),
             pltpu.VMEM((NY, NX - 1, *code), i16),
             pltpu.VMEM((NY, NX - 1, *code), i16),
             pltpu.VMEM((NY, TI * TJ, 8, 128), f32),
@@ -299,18 +335,31 @@
             pltpu.VMEM((2, 1, 128), f32),
             pltpu.VMEM((NX - 1, 1, 128), f32),
             pltpu.VMEM((NY - 1, 1, 128), f32),
-            dma((2,)), dma((3,)), dma((NY,)), dma((NY,)), dma, dma((NY,)),
+            dma((2,)), dma((3,)), dma, dma, pltpu.SemaphoreType.REGULAR((5,)), dma((NY,)), dma((NY,)), dma, dma((NY,)),
             dma((NY - 1,)), dma((NY - 1,)), dma((ZC - 1,)), dma((ZC - 1,)),
             dma((NX - 1,)), dma((NX - 1,)), dma((NY - 1,)), dma((NY - 1,)),
         ],
         compiler_params=pltpu.CompilerParams(collective_id=0, has_side_effects=True),
+        name="exchange",
     )(
         partials.reshape(NY, TI, 8, partials.shape[2]),
-        scales.reshape(NY, TI, 8, scales.shape[2]),
+        scales.reshape(scales.shape[1:]).T,
         overflow_pos,
-        weights,
         exponent.reshape(1),
     )
+    grad, block_scale, master, new_exponent, count = pl.pallas_call(
+        finish,
+        out_shape=(
+            jax.ShapeDtypeStruct((1, 2 * HALF), f32),
+            jax.ShapeDtypeStruct((1, TJ), f32),
+            jax.ShapeDtypeStruct((1, 2 * HALF), f32),
+            jax.ShapeDtypeStruct((1,), jnp.int32),
+            jax.ShapeDtypeStruct((1,), jnp.int32),
+        ),
+        in_specs=[vmem, vmem],
+        out_specs=[vmem, vmem, vmem, smem, smem],
+        name="finish",
+    )(sums, weights)
     return grad, block_scale, master, new_exponent.reshape(()), count.reshape(())
 
 

time: 56.5 us -> 48.3 us (0.85)
  local copies, waits for them, and re-layouts: 5.11 us -> 0 us
  between operations: 5.44 us -> 1.93 us
  Pallas kernels: 45.5 us -> 46.1 us
    unnamed x4 -> x0, local copies, waits for them, and re-layouts: 5.11 us -> none
    pallas_call x1 -> x2, Pallas kernels: 45.5 us -> 46.1 us  [the longest x1 44.6 us: on_device(): pl.pallas_call(kernel, out_shape=jax.ShapeDtypeStruct((16, 128), f32), in...]
where the time goes in v2:
time: 48.3 us; the launch traced here: 48 us
  Pallas kernels  46.1 us (95%)
  between operations  1.93 us (4%)
    pallas_call x1, Pallas kernels, on_device(): pl.pallas_call(kernel, out_shape=jax.ShapeDtypeStruct((16, 128), f32), in...  44.6 us
    pallas_call x1, Pallas kernels, on_device(): pl.pallas_call(finish, out_shape=(jax.ShapeDtypeStruct((1, 2 * HALF), f32...  1.49 us

profile of v2, /device:TPU:1, one launch (start us, length us, event | category | flops | bytes accessed | tf_op | source)
XLA Modules:
  0.0 48.0 jit_solution(17440835469378482066)
XLA Ops:
  1.9 44.6 %exchange.1.sums = f32[16,128]{1,0:T(8,128)} custom-call(bf16[8,3,8,5120]{3,2,1,0:T(8,128)(2,1)} %bitcast.8, bf16[20,192]{1,0:T(8,128)(2,1)} %bitcast.9, s32[1,1]{1,0:T(1,128)S(6)} %copy.10.pos, s32[1]{0:T(128)} %bitcast.7.exponent), custom_call_target="tpu_custom_call" | custom-call | tf_op jit(solution)/shard_map/exchange/pallas_call | solution.py:315
  46.5 1.5 %finish.1 = (f32[1,1280]{1,0:T(1,128)}, f32[1,5]{1,0:T(1,128)}, f32[1,1280]{1,0:T(1,128)}, s32[1]{0:T(128)}, s32[1]{0:T(128)}) custom-call(f32[16,128]{1,0:T(8,128)} %exchange.1.sums, f32[1,1280]{1,0:T(1,128)} %weights.1), custom_call_target="tpu_custom_call" | custom-call | tf_op jit(solution)/shard_map/finish/pallas_call | solution.py:350

commit v3 on v2

v3 whole, which is shorter than its diff:
```python
import functools

import jax
import jax.numpy as jnp
from jax import lax
from jax.experimental import pallas as pl
from jax.experimental.pallas import tpu as pltpu
from jax.sharding import PartitionSpec as P

MESH = pl.DeviceIdType.MESH
NX, NY, NZ = 4, 8, 12
ZC = 2 * NZ
TI, TJ = ZC // 8, 5
HALF = TJ * 128
NB = 3
TOP = 32767.0
NS = NY - 3
FLAG_STEP = 3


def wait(ref, sem):
    pltpu.make_async_copy(ref, ref, sem).wait()


def far_first(k, n):
    m = (k + 1) // 2
    return jnp.where(k % 2 == 1, n // 2 - m, n // 2 + m)


def top_of(row):
    peak = functools.reduce(jnp.maximum, [jnp.abs(t) for t in row])
    peak = jnp.maximum(jnp.max(peak, axis=1, keepdims=True), 1e-30)
    return jnp.ceil(jnp.log2(jnp.broadcast_to(peak, (8, 128))) + 1e-3)


def code(values):
    return jnp.round(values).astype(jnp.int32).astype(jnp.int16)


def encode(tiles, tops, out):
    lane = lax.broadcasted_iota(jnp.int32, (8, 128), 1)
    flat, marks = [], jnp.zeros((8, 128), jnp.float32)
    for i in range(TI):
        factor = jnp.exp2(-tops[i]) * TOP
        flat += [t * factor for t in tiles[i]]
        marks = jnp.where(lane == i, tops[i], marks)
    flat.append(marks)
    for p in range(len(flat) // 2):
        out[p] = code(jnp.concatenate([flat[2 * p], flat[2 * p + 1]], axis=0))


def decode(ref):
    flat = []
    for p in range((TI * TJ + 1) // 2):
        pair = ref[p].astype(jnp.int32).astype(jnp.float32)
        flat += [pair[:8], pair[8:]]
    factors = jnp.exp2(flat[TI * TJ]) * (1.0 / TOP)
    return [
        [flat[i * TJ + j] * jnp.broadcast_to(factors[:, i : i + 1], (8, 128)) for j in range(TJ)]
        for i in range(TI)
    ]


def add(a, b):
    return [[p + q for p, q in zip(r, s)] for r, s in zip(a, b)]


def kernel(
    part, scales, pos, exponent, weights,
    out,
    lev, par, sc, st, turned, bx, flag, power, held, terms, cs, ms, xr, mr, ys, yr, zs, zq, zr, fs, fx, fy, fz,
    load_sem, sc_sem, flag_sem, power_sem, held_sem, near, core_send, core_recv, x_send, x_recv, m_send, m_recv, y_send, y_recv, z_send, z_recv,
    fx_send, fx_recv, fy_send, fy_recv, fz_send, fz_recv,
):
    inter, x = lax.axis_index("inter"), lax.axis_index("intra")
    c, zc = inter % 2, inter % ZC
    z, y = zc // 2, inter // ZC
    partner = inter + 1 - 2 * c

    for h, side in ((1, 1 - c), (0, c)):
        for xt in range(NX):
            columns = pl.ds(pl.multiple_of(xt * 2 * HALF + side * HALF, 128), HALF)
            pltpu.make_async_copy(part.at[:, :, :, columns], lev.at[h, :, xt], load_sem.at[h]).start()
    pltpu.make_async_copy(scales, sc.at[0], sc_sem.at[0]).start()

    pltpu.make_async_copy(pos, flag, flag_sem).start()
    pltpu.make_async_copy(exponent, power, power_sem).start()
    pltpu.make_async_copy(weights, held, held_sem).start()

    barrier = pltpu.get_barrier_semaphore()

    def along_y(d):
        return ((y + d) % NY * ZC + zc, x)

    def along_z(d):
        return (y * ZC + (zc + 2 * d) % ZC, x)

    def tell(sem, to):
        pl.semaphore_signal(sem, inc=1, device_id=to, device_id_type=MESH)

    def tell_both(sem, along, n, d):
        tell(near.at[sem], along(d))
        tell(near.at[sem], along(n - d))

    tell(barrier, (partner, x))
    for d in range(1, NX):
        tell(barrier, (inter, (x + d) % NX))
    for d in (1, NY - 1):
        tell(barrier, along_y(d))
    for d in (1, NZ - 1):
        tell(barrier, along_z(d))
    with jax.named_scope("load"):
        wait(sc.at[0], sc_sem.at[0])
        wait(lev.at[1], load_sem.at[1])
    with jax.named_scope("barrier"):
        pl.semaphore_wait(barrier, 1 + NX - 1 + 2 + 2)
    tell_both(0, along_y, NY, 1)
    tell_both(1, along_z, NZ, 1)

    def offset(q):
        late = far_first(q - 2, NY)
        return jnp.where(q == 0, NY // 2, jnp.where(q == 1, 1, jnp.where(q == 2, NY - 1, jnp.where(q == NY - 1, 0, late))))

    def core_copy(k):
        yt = (y + offset(k)) % NY
        return pltpu.make_async_remote_copy(
            lev.at[1, yt], par.at[yt], core_send, core_recv.at[k], (partner, x), MESH
        )

    scale_copy = pltpu.make_async_remote_copy(
        sc.at[0], sc.at[1], sc_sem.at[1], sc_sem.at[2], (partner, x), MESH
    )
    scale_copy.start()

    @pl.loop(0, NY)
    def _(k):
        core_copy(k).start()

    def flag_x(d):
        return pltpu.make_async_remote_copy(
            fs.at[0], fx.at[d - 1], fx_send.at[d - 1], fx_recv.at[d - 1], (inter, (x + d) % NX), MESH
        )

    wait(flag, flag_sem)
    wait(power, power_sem)
    fs[0] = jnp.full((1, 128), (flag[0, 0] >= 0).astype(jnp.float32), jnp.float32)
    for d in range(1, NX):
        flag_x(d).start()

    def turn(h):
        st[:20, : NY * ZC] = sc[h].astype(jnp.float32)
        turned[h] = st[...].T[: NY * ZC]

    block = lax.broadcasted_iota(jnp.int32, (32, 128), 0)

    def spread(h, first, n):
        rows = turned[h, pl.ds(pl.multiple_of(first * 8, 8), n * 8), :].astype(jnp.bfloat16)
        for t in range(0, NB * NX, 2):
            picks = [
                jnp.where(block == u // NB * TJ + 2 * c + u % NB, 1.0, 0.0).astype(jnp.bfloat16)
                for u in (t, t + 1)
            ]
            both = jnp.dot(rows, jnp.concatenate(picks, axis=1), preferred_element_type=jnp.float32)
            for u in range(2):
                bx[h, pl.ds(first, n), t + u] = both[:, u * 128 : (u + 1) * 128].reshape(n, 8, 128)

    st[...] = jnp.zeros((32, 256), jnp.float32)
    with jax.named_scope("spread0"):
        turn(0)
        spread(0, 0, NY * TI)
    with jax.named_scope("wait_scale"):
        wait(lev.at[0], load_sem.at[0])
        scale_copy.wait()
    with jax.named_scope("turn"):
        turn(1)

    def x_copy(src, k, d):
        return pltpu.make_async_remote_copy(
            src, xr.at[k, d - 1], x_send, x_recv.at[k], (inter, (x + d) % NX), MESH
        )

    def near_copy(q):
        return pltpu.make_async_remote_copy(
            cs.at[q], mr.at[q - 1], m_send, m_recv.at[q - 1], along_y(offset(q)), MESH
        )

    def tiles_of(q, d):
        return [[terms[q, d, i * TJ + j] for j in range(TJ)] for i in range(TI)]

    @pl.loop(0, NY)
    def _(q):
        yt = (y + offset(q)) % NY
        spread(1, yt * TI, TI)
        with jax.named_scope("wait_core"):
            wait(par.at[yt], core_recv.at[q])
        tops = []
        for d in range(NX):
            xt = (x + d) % NX
            for i in range(TI):
                row = None
                for h in range(2):
                    b = [bx[h, yt * TI + i, xt * NB + n] for n in range(NB)]
                    even = c == 0
                    b = [b[0], jnp.where(even, b[0], b[1]), b[1], jnp.where(even, b[1], b[2]), b[2]]
                    levels = lev[0, yt, xt, i] if h == 0 else par[yt, xt, i]
                    levels = levels.astype(jnp.float32)
                    term = [levels[:, j * 128 : (j + 1) * 128] * b[j] for j in range(TJ)]
                    row = term if row is None else [p + q for p, q in zip(row, term)]
                for j in range(TJ):
                    terms[q, d, i * TJ + j] = row[j]
                tops.append(top_of(row))

        def send(d):
            encode(tiles_of(q, d), tops[d * TI : d * TI + TI], cs.at[q, d])

        near_by = jnp.logical_or(q == 1, q == 2)

        @pl.when(near_by)
        def _():
            for d in range(NX):
                send(d)
            near_copy(q).start()

        @pl.when(jnp.logical_not(jnp.logical_or(near_by, q == NY - 1)))
        def _():
            for d in (2, 1, 3):
                send(d)
                x_copy(cs.at[q, d], jnp.where(q == 0, 0, q - 2), d).start()

    with jax.named_scope("near0"):
        pl.semaphore_wait(near.at[0], 2)
        pl.semaphore_wait(near.at[1], 2)
    tell_both(2, along_y, NY, 2)
    tell_both(3, along_z, NZ, 2)

    flags = fs[0]
    for d in range(1, NX):
        wait(fx.at[d - 1], fx_recv.at[d - 1])
        flags = flags + fx[d - 1]
    fs[1] = flags
    with jax.named_scope("near"):
        pl.semaphore_wait(near.at[2], 2)
        pl.semaphore_wait(near.at[3], 2)
    tell_both(4, along_z, NZ, 4)

    def flag_y(d):
        return pltpu.make_async_remote_copy(
            fs.at[1], fy.at[d - 1], fy_send.at[d - 1], fy_recv.at[d - 1], along_y(d), MESH
        )

    for d in range(1, NY):
        flag_y(d).start()

    def y_copy(k):
        return pltpu.make_async_remote_copy(
            ys.at[k], yr.at[k], y_send, y_recv.at[k], along_y(far_first(k, NY)), MESH
        )

    def x_sum(k, q):
        with jax.named_scope("wait_x"):
            wait(xr.at[k], x_recv.at[k])
        tiles = tiles_of(q, 0)
        for d in range(1, NX):
            tiles = add(tiles, decode(xr.at[k, d - 1]))
        return tiles

    def flag_z(k):
        to = (zc + far_first(k, ZC)) % ZC
        return pltpu.make_async_remote_copy(
            fs.at[2], fz.at[zc], fz_send, fz_recv, (y * ZC + to, x), MESH
        )

    def pass_on(k, q):
        tiles = x_sum(k, q)
        encode(tiles, [top_of(row) for row in tiles], ys.at[k])
        y_copy(k).start()

    pass_on(0, 0)

    with jax.named_scope("wait_m"):
        for n in range(2):
            wait(mr.at[n], m_recv.at[n])
    for d in (2, 1, 3, 0):
        tiles = add(add(tiles_of(NY - 1, d), decode(mr.at[0, d])), decode(mr.at[1, d]))
        if d:
            encode(tiles, [top_of(row) for row in tiles], ms.at[d - 1])
            x_copy(ms.at[d - 1], NS, d).start()
        else:
            for i in range(TI):
                for j in range(TJ):
                    terms[NY - 1, 0, i * TJ + j] = tiles[i][j]

    @pl.loop(1, NS)
    def _(k):
        pass_on(k, k + 2)

        @pl.when(k == FLAG_STEP)
        def _():
            flags = fs[1]
            with jax.named_scope("wait_fy"):
                for d in range(1, NY):
                    wait(fy.at[d - 1], fy_recv.at[d - 1])
                    flags = flags + fy[d - 1]
            fs[2] = flags
            fz[zc] = flags
            with jax.named_scope("near4"):
                pl.semaphore_wait(near.at[4], 2)

            @pl.loop(0, ZC - 1)
            def _(n):
                flag_z(n).start()

    tiles = x_sum(NS, NY - 1)
    for k in range(NS):
        with jax.named_scope("wait_y"):
            wait(yr.at[k], y_recv.at[k])
        tiles = add(tiles, decode(yr.at[k]))
    for i in range(TI):
        top = top_of(tiles[i])
        factor = jnp.exp2(-top) * TOP
        for j in range(TJ):
            zs[pl.ds(i * 64 + j, 8, stride=8), :] = tiles[i][j] * factor
        zs[pl.ds(i * 64 + TJ, 8, stride=8), :] = top
    for r in range(ZC):
        zq[r] = code(zs[r * 8 : r * 8 + 8, :])

    def z_copy(k):
        to = (zc + far_first(k, ZC)) % ZC
        return pltpu.make_async_remote_copy(
            zq.at[to, : TJ + 1], zr.at[zc, : TJ + 1], z_send, z_recv, (y * ZC + to, x), MESH
        )

    @pl.loop(0, ZC - 1)
    def _(k):
        z_copy(k).start()

    zr[zc] = zq[zc]

    wait(held, held_sem)
    for h in range(2):
        for j in range(TJ):
            at = (h * TJ + j) * 128
            out[16 + h * 8 + j : 17 + h * 8 + j, :] = held[:, at : at + 128]

    for d in range(1, NX):
        wait(fs.at[0], fx_send.at[d - 1])
    for d in range(1, NY):
        wait(fs.at[1], fy_send.at[d - 1])
    wait(lev.at[1], core_send)
    wait(xr, x_send)
    wait(mr, m_send)
    wait(ys, y_send)
    wait(fz.at[: ZC - 1], fz_send)
    with jax.named_scope("wait_flags"):
        wait(fz.at[: ZC - 1], fz_recv)
    count = functools.reduce(jnp.add, [fz[n] for n in range(ZC)])
    with jax.named_scope("wait_z"):
        wait(zr.at[: ZC - 1, : TJ + 1], z_recv)
    wait(zr.at[: ZC - 1, : TJ + 1], z_send)
    for h in range(2):
        total = None
        for n in range(NZ):
            codes = zr[2 * n + h].astype(jnp.int32).astype(jnp.float32)
            part_sum = codes * (jnp.exp2(jnp.broadcast_to(codes[TJ : TJ + 1], (8, 128))) * (1.0 / TOP))
            total = part_sum if total is None else total + part_sum
        out[h * 8 : h * 8 + TJ, :] = total[:TJ]
    out[TJ : TJ + 1, :] = count
    out[7:8, :] = jnp.full((1, 128), power[0].astype(jnp.float32), jnp.float32)


def finish(sums, grad, block_scale, master, new_exponent, count):
    flagged = sums[TJ, 0].astype(jnp.int32)
    factor = jnp.exp2(-jnp.broadcast_to(sums[7:8, :], (8, 128)))
    peaks = []
    for h in range(2):
        g = sums[h * 8 : h * 8 + 8, :] * factor
        peak = jnp.max(jnp.abs(g), axis=1, keepdims=True)
        for j in range(TJ):
            at = slice((h * TJ + j) * 128, (h * TJ + j + 1) * 128)
            w = sums[16 + h * 8 + j : 17 + h * 8 + j, :]
            grad[:, at] = g[j : j + 1]
            master[:, at] = jnp.where(flagged == 0, w - 0.5 * g[j : j + 1], w)
            peaks.append(peak[j : j + 1])
    lane = lax.broadcasted_iota(jnp.int32, (1, 128), 1)
    scale = jnp.zeros((1, 128), jnp.float32)
    for b in range(TJ):
        top = jnp.maximum(peaks[2 * b], peaks[2 * b + 1]) / 127.0
        scale = jnp.where(lane == b, jnp.broadcast_to(top, (1, 128)), scale)
    block_scale[...] = scale[:, :TJ]
    new_exponent[0] = sums[7, 0].astype(jnp.int32) - (flagged > 0).astype(jnp.int32)
    count[0] = flagged


def on_device(partials, scales, overflow_pos, weights, exponent):
    vmem, smem, hbm = (
        pl.BlockSpec(memory_space=m) for m in (pltpu.VMEM, pltpu.SMEM, pltpu.HBM)
    )
    f32, i16, dma = jnp.float32, jnp.int16, pltpu.SemaphoreType.DMA
    codes = (8, 16, 128)
    sums = pl.pallas_call(
        kernel,
        out_shape=pltpu.VMEM((32, 128), f32),
        in_specs=[hbm] * 5,
        out_specs=vmem,
        scratch_shapes=[
            pltpu.VMEM((2, NY, NX, TI, 8, HALF), jnp.bfloat16),
            pltpu.VMEM((NY, NX, TI, 8, HALF), jnp.bfloat16),
            pltpu.VMEM((2, 20, NY * ZC), jnp.bfloat16),
            pltpu.VMEM((32, 256), f32),
            pltpu.VMEM((2, NY * ZC, 32), f32),
            pltpu.VMEM((2, NY * TI, NB * NX, 8, 128), f32),
            pltpu.SMEM((1, 1), jnp.int32),
            pltpu.SMEM((1,), jnp.int32),
            pltpu.VMEM((1, 2 * HALF), f32),
            pltpu.VMEM((NY, NX, TI * TJ, 8, 128), f32),
            pltpu.VMEM((NY - 1, NX, *codes), i16),
            pltpu.VMEM((NX - 1, *codes), i16),
            pltpu.VMEM((NS + 1, NX - 1, *codes), i16),
            pltpu.VMEM((2, NX, *codes), i16),
            pltpu.VMEM((NS, *codes), i16),
            pltpu.VMEM((NS, *codes), i16),
            pltpu.VMEM((ZC * 8, 128), f32),
            pltpu.VMEM((ZC, 8, 128), i16),
            pltpu.VMEM((ZC, 8, 128), i16),
            pltpu.VMEM((3, 1, 128), f32),
            pltpu.VMEM((NX - 1, 1, 128), f32),
            pltpu.VMEM((NY - 1, 1, 128), f32),
            pltpu.VMEM((ZC, 1, 128), f32),
            dma((2,)), dma((3,)), dma, dma, dma, pltpu.SemaphoreType.REGULAR((5,)), dma, dma((NY,)), dma, dma((NS + 1,)),
            dma, dma((2,)), dma, dma((NS,)), dma, dma,
            dma((NX - 1,)), dma((NX - 1,)), dma((NY - 1,)), dma((NY - 1,)), dma, dma,
        ],
        compiler_params=pltpu.CompilerParams(collective_id=0, has_side_effects=True),
        name="exchange",
    )(
        partials.reshape(NY, TI, 8, partials.shape[2]),
        scales.reshape(scales.shape[1:]).T,
        overflow_pos,
        exponent.reshape(1),
        weights,
    )
    grad, block_scale, master, new_exponent, count = pl.pallas_call(
        finish,
        out_shape=(
            jax.ShapeDtypeStruct((1, 2 * HALF), f32),
            jax.ShapeDtypeStruct((1, TJ), f32),
            jax.ShapeDtypeStruct((1, 2 * HALF), f32),
            jax.ShapeDtypeStruct((1,), jnp.int32),
            jax.ShapeDtypeStruct((1,), jnp.int32),
        ),
        in_specs=[vmem],
        out_specs=[vmem, vmem, vmem, smem, smem],
        name="finish",
    )(pltpu.with_memory_space_constraint(sums, pltpu.VMEM))
    return grad, block_scale, master, new_exponent.reshape(()), count.reshape(())


def solution(mesh):
    return jax.shard_map(
        on_device,
        mesh=mesh,
        in_specs=(
            P(("inter", "intra"), None, None),
            P(("inter", "intra"), None, None),
            P(("inter", "intra"), None),
            P("inter", "intra"),
            P(),
        ),
        out_specs=(P("inter", "intra"), P("inter", "intra"), P("inter", "intra"), P(), P()),
        check_vma=False,
    )
```

time: 48.3 us -> 41.2 us (0.85)
  Pallas kernels: 46.1 us -> 39.1 us
    pallas_call x1, Pallas kernels: 44.6 us -> 38.3 us  [on_device(): pl.pallas_call(kernel, out_shape=pltpu.VMEM((32, 128), f32), in_specs=[hb...]
    pallas_call x1, Pallas kernels: 1.49 us -> 0.78 us  [on_device(): pl.pallas_call(finish, out_shape=(jax.ShapeDtypeStruct((1, 2 * HALF), f32...]
where the time goes in v3:
time: 41.2 us; the launch traced here: 41 us
  Pallas kernels  39.1 us (95%)
  between operations  1.93 us (5%)
    pallas_call x1, Pallas kernels, on_device(): pl.pallas_call(kernel, out_shape=pltpu.VMEM((32, 128), f32), in_specs=[hb...  38.3 us

profile of v3, /device:TPU:1, one launch (start us, length us, event | category | flops | bytes accessed | tf_op | source)
XLA Modules:
  0.0 41.0 jit_solution(435781536186335341)
XLA Ops:
  1.9 38.3 %exchange.1.sums = f32[32,128]{1,0:T(8,128)S(1)} custom-call(bf16[8,3,8,5120]{3,2,1,0:T(8,128)(2,1)} %bitcast.8, bf16[20,192]{1,0:T(8,128)(2,1)} %bitcast.9, s32[1,1]{1,0:T(1,128)S(6)} %copy.10.pos, s32[1]{0:T(128)} %bitcast.7.exponent, f32[1,1280]{1,0:T(1,128)} %weights.1), custom_call_target="tpu_custom_call" | custom-call | tf_op jit(solution)/shard_map/exchange/pallas_call | solution.py:400
  40.3 0.8 %finish.1 = (f32[1,1280]{1,0:T(1,128)}, f32[1,5]{1,0:T(1,128)}, f32[1,1280]{1,0:T(1,128)}, s32[1]{0:T(128)}, s32[1]{0:T(128)}) custom-call(f32[32,128]{1,0:T(8,128)S(1)} %exchange.1.sums), custom_call_target="tpu_custom_call" | custom-call | tf_op jit(solution)/shard_map/finish/pallas_call | solution.py:442

commit v4 on v3

--- a/solution.py
+++ b/solution.py
@@ -14,8 +14,8 @@
 HALF = TJ * 128
 NB = 3
 TOP = 32767.0
-NS = NY - 3
-FLAG_STEP = 3
+FULL = 3
+OWN = NY - 1
 
 
 def wait(ref, sem):
@@ -68,24 +68,14 @@
 def kernel(
     part, scales, pos, exponent, weights,
     out,
-    lev, par, sc, st, turned, bx, flag, power, held, terms, cs, ms, xr, mr, ys, yr, zs, zq, zr, fs, fx, fy, fz,
-    load_sem, sc_sem, flag_sem, power_sem, held_sem, near, core_send, core_recv, x_send, x_recv, m_send, m_recv, y_send, y_recv, z_send, z_recv,
+    lev, par, sc, st, turned, bx, flag, power, held, terms, cs, xr, dr, ys, yr, zs, zq, zr, fs, fx, fy, fz,
+    load_sem, sc_sem, flag_sem, power_sem, held_sem, near, core_send, core_recv, x_send, x_recv, d_send, d_recv, y_send, y_recv, z_send, z_recv,
     fx_send, fx_recv, fy_send, fy_recv, fz_send, fz_recv,
 ):
     inter, x = lax.axis_index("inter"), lax.axis_index("intra")
     c, zc = inter % 2, inter % ZC
     z, y = zc // 2, inter // ZC
     partner = inter + 1 - 2 * c
-
-    for h, side in ((1, 1 - c), (0, c)):
-        for xt in range(NX):
-            columns = pl.ds(pl.multiple_of(xt * 2 * HALF + side * HALF, 128), HALF)
-            pltpu.make_async_copy(part.at[:, :, :, columns], lev.at[h, :, xt], load_sem.at[h]).start()
-    pltpu.make_async_copy(scales, sc.at[0], sc_sem.at[0]).start()
-
-    pltpu.make_async_copy(pos, flag, flag_sem).start()
-    pltpu.make_async_copy(exponent, power, power_sem).start()
-    pltpu.make_async_copy(weights, held, held_sem).start()
 
     barrier = pltpu.get_barrier_semaphore()
 
@@ -109,6 +99,16 @@
         tell(barrier, along_y(d))
     for d in (1, NZ - 1):
         tell(barrier, along_z(d))
+    for h, side in ((1, 1 - c), (0, c)):
+        for xt in range(NX):
+            columns = pl.ds(pl.multiple_of(xt * 2 * HALF + side * HALF, 128), HALF)
+            pltpu.make_async_copy(part.at[:, :, :, columns], lev.at[h, :, xt], load_sem.at[h]).start()
+    pltpu.make_async_copy(scales, sc.at[0], sc_sem.at[0]).start()
+
+    pltpu.make_async_copy(pos, flag, flag_sem).start()
+    pltpu.make_async_copy(exponent, power, power_sem).start()
+    pltpu.make_async_copy(weights, held, held_sem).start()
+
     with jax.named_scope("load"):
         wait(sc.at[0], sc_sem.at[0])
         wait(lev.at[1], load_sem.at[1])
@@ -118,8 +118,7 @@
     tell_both(1, along_z, NZ, 1)
 
     def offset(q):
-        late = far_first(q - 2, NY)
-        return jnp.where(q == 0, NY // 2, jnp.where(q == 1, 1, jnp.where(q == 2, NY - 1, jnp.where(q == NY - 1, 0, late))))
+        return far_first(q, NY)
 
     def core_copy(k):
         yt = (y + offset(k)) % NY
@@ -176,21 +175,22 @@
 
     def x_copy(src, k, d):
         return pltpu.make_async_remote_copy(
-            src, xr.at[k, d - 1], x_send, x_recv.at[k], (inter, (x + d) % NX), MESH
-        )
-
-    def near_copy(q):
-        return pltpu.make_async_remote_copy(
-            cs.at[q], mr.at[q - 1], m_send, m_recv.at[q - 1], along_y(offset(q)), MESH
+            src, xr.at[k, d - 1], x_send.at[k, d - 1], x_recv.at[k, d - 1], (inter, (x + d) % NX), MESH
+        )
+
+    def early_copy(q):
+        return pltpu.make_async_remote_copy(
+            cs.at[q, 2], dr.at[q - FULL], d_send, d_recv.at[q - FULL], along_y(offset(q)), MESH
         )
 
     def tiles_of(q, d):
         return [[terms[q, d, i * TJ + j] for j in range(TJ)] for i in range(TI)]
 
-    @pl.loop(0, NY)
-    def _(q):
+    with jax.named_scope("spread1"):
+        spread(1, (y + offset(0)) % NY * TI, TI)
+
+    def produce(q):
         yt = (y + offset(q)) % NY
-        spread(1, yt * TI, TI)
         with jax.named_scope("wait_core"):
             wait(par.at[yt], core_recv.at[q])
         tops = []
@@ -213,25 +213,35 @@
         def send(d):
             encode(tiles_of(q, d), tops[d * TI : d * TI + TI], cs.at[q, d])
 
-        near_by = jnp.logical_or(q == 1, q == 2)
-
-        @pl.when(near_by)
+        @pl.when(q < FULL)
         def _():
-            for d in range(NX):
-                send(d)
-            near_copy(q).start()
-
-        @pl.when(jnp.logical_not(jnp.logical_or(near_by, q == NY - 1)))
+            send(2)
+            x_copy(cs.at[q, 2], q, 2).start()
+
+        @pl.when(jnp.logical_and(q >= FULL, q < OWN))
         def _():
-            for d in (2, 1, 3):
-                send(d)
-                x_copy(cs.at[q, d], jnp.where(q == 0, 0, q - 2), d).start()
-
-    with jax.named_scope("near0"):
-        pl.semaphore_wait(near.at[0], 2)
-        pl.semaphore_wait(near.at[1], 2)
-    tell_both(2, along_y, NY, 2)
-    tell_both(3, along_z, NZ, 2)
+            send(2)
+            early_copy(q).start()
+
+        for d in (1, 3):
+            send(d)
+            x_copy(cs.at[q, d], q, d).start()
+
+        @pl.when(q == FULL - 1)
+        def _():
+            with jax.named_scope("near0"):
+                pl.semaphore_wait(near.at[0], 2)
+                pl.semaphore_wait(near.at[1], 2)
+            tell_both(2, along_y, NY, 2)
+            tell_both(3, along_z, NZ, 2)
+
+    @pl.loop(0, NY)
+    def _(q):
+        produce(q)
+
+        @pl.when(q == 0)
+        def _():
+            spread(1, 0, NY * TI)
 
     flags = fs[0]
     for d in range(1, NX):
@@ -253,14 +263,15 @@
 
     def y_copy(k):
         return pltpu.make_async_remote_copy(
-            ys.at[k], yr.at[k], y_send, y_recv.at[k], along_y(far_first(k, NY)), MESH
-        )
-
-    def x_sum(k, q):
+            ys.at[k], yr.at[k], y_send, y_recv.at[k], along_y(offset(k)), MESH
+        )
+
+    def x_sum(k, sides):
         with jax.named_scope("wait_x"):
-            wait(xr.at[k], x_recv.at[k])
-        tiles = tiles_of(q, 0)
-        for d in range(1, NX):
+            for d in sides:
+                wait(xr.at[k, d - 1], x_recv.at[k, d - 1])
+        tiles = tiles_of(k, 0)
+        for d in sides:
             tiles = add(tiles, decode(xr.at[k, d - 1]))
         return tiles
 
@@ -270,48 +281,45 @@
             fs.at[2], fz.at[zc], fz_send, fz_recv, (y * ZC + to, x), MESH
         )
 
-    def pass_on(k, q):
-        tiles = x_sum(k, q)
+    def pass_on(k, sides):
+        tiles = x_sum(k, sides)
         encode(tiles, [top_of(row) for row in tiles], ys.at[k])
         y_copy(k).start()
 
-    pass_on(0, 0)
-
-    with jax.named_scope("wait_m"):
-        for n in range(2):
-            wait(mr.at[n], m_recv.at[n])
-    for d in (2, 1, 3, 0):
-        tiles = add(add(tiles_of(NY - 1, d), decode(mr.at[0, d])), decode(mr.at[1, d]))
-        if d:
-            encode(tiles, [top_of(row) for row in tiles], ms.at[d - 1])
-            x_copy(ms.at[d - 1], NS, d).start()
-        else:
-            for i in range(TI):
-                for j in range(TJ):
-                    terms[NY - 1, 0, i * TJ + j] = tiles[i][j]
-
-    @pl.loop(1, NS)
+    @pl.loop(0, FULL - 1)
     def _(k):
-        pass_on(k, k + 2)
-
-        @pl.when(k == FLAG_STEP)
-        def _():
-            flags = fs[1]
-            with jax.named_scope("wait_fy"):
-                for d in range(1, NY):
-                    wait(fy.at[d - 1], fy_recv.at[d - 1])
-                    flags = flags + fy[d - 1]
-            fs[2] = flags
-            fz[zc] = flags
-            with jax.named_scope("near4"):
-                pl.semaphore_wait(near.at[4], 2)
-
-            @pl.loop(0, ZC - 1)
-            def _(n):
-                flag_z(n).start()
-
-    tiles = x_sum(NS, NY - 1)
-    for k in range(NS):
+        pass_on(k, (1, 3, 2))
+
+    tiles = tiles_of(OWN, 2)
+    for n in range(OWN - FULL):
+        with jax.named_scope("wait_d"):
+            wait(dr.at[n], d_recv.at[n])
+        tiles = add(tiles, decode(dr.at[n]))
+    encode(tiles, [top_of(row) for row in tiles], cs.at[OWN, 2])
+    x_copy(cs.at[OWN, 2], OWN, 2).start()
+
+    pass_on(FULL - 1, (1, 3, 2))
+
+    @pl.loop(FULL, OWN)
+    def _(k):
+        pass_on(k, (1, 3))
+
+    flags = fs[1]
+    with jax.named_scope("wait_fy"):
+        for d in range(1, NY):
+            wait(fy.at[d - 1], fy_recv.at[d - 1])
+            flags = flags + fy[d - 1]
+    fs[2] = flags
+    fz[zc] = flags
+    with jax.named_scope("near4"):
+        pl.semaphore_wait(near.at[4], 2)
+
+    @pl.loop(0, ZC - 1)
+    def _(n):
+        flag_z(n).start()
+
+    tiles = x_sum(OWN, (1, 3, 2))
+    for k in range(OWN):
         with jax.named_scope("wait_y"):
             wait(yr.at[k], y_recv.at[k])
         tiles = add(tiles, decode(yr.at[k]))
@@ -347,8 +355,10 @@
     for d in range(1, NY):
         wait(fs.at[1], fy_send.at[d - 1])
     wait(lev.at[1], core_send)
-    wait(xr, x_send)
-    wait(mr, m_send)
+    for k in range(NY):
+        for d in (1, 3) if FULL <= k < OWN else (1, 2, 3):
+            wait(xr.at[k, d - 1], x_send.at[k, d - 1])
+    wait(dr, d_send)
     wait(ys, y_send)
     wait(fz.at[: ZC - 1], fz_send)
     with jax.named_scope("wait_flags"):
@@ -413,12 +423,11 @@
             pltpu.SMEM((1,), jnp.int32),
             pltpu.VMEM((1, 2 * HALF), f32),
             pltpu.VMEM((NY, NX, TI * TJ, 8, 128), f32),
-            pltpu.VMEM((NY - 1, NX, *codes), i16),
-            pltpu.VMEM((NX - 1, *codes), i16),
-            pltpu.VMEM((NS + 1, NX - 1, *codes), i16),
-            pltpu.VMEM((2, NX, *codes), i16),
-            pltpu.VMEM((NS, *codes), i16),
-            pltpu.VMEM((NS, *codes), i16),
+            pltpu.VMEM((NY, NX, *codes), i16),
+            pltpu.VMEM((NY, NX - 1, *codes), i16),
+            pltpu.VMEM((OWN - FULL, *codes), i16),
+            pltpu.VMEM((OWN, *codes), i16),
+            pltpu.VMEM((OWN, *codes), i16),
             pltpu.VMEM((ZC * 8, 128), f32),
             pltpu.VMEM((ZC, 8, 128), i16),
             pltpu.VMEM((ZC, 8, 128), i16),
@@ -426,8 +435,8 @@
             pltpu.VMEM((NX - 1, 1, 128), f32),
             pltpu.VMEM((NY - 1, 1, 128), f32),
             pltpu.VMEM((ZC, 1, 128), f32),
-            dma((2,)), dma((3,)), dma, dma, dma, pltpu.SemaphoreType.REGULAR((5,)), dma, dma((NY,)), dma, dma((NS + 1,)),
-            dma, dma((2,)), dma, dma((NS,)), dma, dma,
+            dma((2,)), dma((3,)), dma, dma, dma, pltpu.SemaphoreType.REGULAR((5,)), dma, dma((NY,)), dma((NY, NX - 1)), dma((NY, NX - 1)),
+            dma, dma((OWN - FULL,)), dma, dma((OWN,)), dma, dma,
             dma((NX - 1,)), dma((NX - 1,)), dma((NY - 1,)), dma((NY - 1,)), dma, dma,
         ],
         compiler_params=pltpu.CompilerParams(collective_id=0, has_side_effects=True),

time: 41.2 us -> 41.1 us (level)
  no operation moved by 1% of the time
where the time goes in v4:
time: 41.1 us; the launch traced here: 40.9 us
  Pallas kernels  39 us (95%)
  between operations  1.93 us (5%)
    pallas_call x1, Pallas kernels, on_device(): pl.pallas_call(kernel, out_shape=pltpu.VMEM((32, 128), f32), in_specs=[hb...  38.2 us

profile of v4, /device:TPU:1, one launch (start us, length us, event | category | flops | bytes accessed | tf_op | source)
XLA Modules:
  0.0 40.9 jit_solution(13897919301863929245)
XLA Ops:
  1.9 38.2 %exchange.1.sums = f32[32,128]{1,0:T(8,128)S(1)} custom-call(bf16[8,3,8,5120]{3,2,1,0:T(8,128)(2,1)} %bitcast.8, bf16[20,192]{1,0:T(8,128)(2,1)} %bitcast.9, s32[1,1]{1,0:T(1,128)S(6)} %copy.10.pos, s32[1]{0:T(128)} %bitcast.7.exponent, f32[1,1280]{1,0:T(1,128)} %weights.1), custom_call_target="tpu_custom_call" | custom-call | tf_op jit(solution)/shard_map/exchange/pallas_call | solution.py:410
  40.1 0.8 %finish.1 = (f32[1,1280]{1,0:T(1,128)}, f32[1,5]{1,0:T(1,128)}, f32[1,1280]{1,0:T(1,128)}, s32[1]{0:T(128)}, s32[1]{0:T(128)}) custom-call(f32[32,128]{1,0:T(8,128)S(1)} %exchange.1.sums), custom_call_target="tpu_custom_call" | custom-call | tf_op jit(solution)/shard_map/finish/pallas_call | solution.py:451

commit v5 on v4

--- a/solution.py
+++ b/solution.py
@@ -14,8 +14,11 @@
 HALF = TJ * 128
 NB = 3
 TOP = 32767.0
+USED = TI * TJ * 8 + 2
 FULL = 3
 OWN = NY - 1
+SIDES = (1, 3, 2)
+SENT = 3 * (FULL + 1) + 2 * (OWN - FULL) + OWN - FULL + OWN
 
 
 def wait(ref, sem):
@@ -37,28 +40,34 @@
     return jnp.round(values).astype(jnp.int32).astype(jnp.int16)
 
 
+def row_lane(i):
+    lane = lax.broadcasted_iota(jnp.int32, (8, 128), 1)
+    return lane == lax.broadcasted_iota(jnp.int32, (8, 128), 0) + 8 * i
+
+
 def encode(tiles, tops, out):
-    lane = lax.broadcasted_iota(jnp.int32, (8, 128), 1)
     flat, marks = [], jnp.zeros((8, 128), jnp.float32)
     for i in range(TI):
         factor = jnp.exp2(-tops[i]) * TOP
         flat += [t * factor for t in tiles[i]]
-        marks = jnp.where(lane == i, tops[i], marks)
-    flat.append(marks)
+        marks = jnp.where(row_lane(i), tops[i], marks)
+    flat.append(jnp.broadcast_to(jnp.sum(marks, axis=0, keepdims=True), (8, 128)))
     for p in range(len(flat) // 2):
-        out[p] = code(jnp.concatenate([flat[2 * p], flat[2 * p + 1]], axis=0))
+        out[p * 16 : p * 16 + 16, :] = code(jnp.concatenate([flat[2 * p], flat[2 * p + 1]], axis=0))
 
 
 def decode(ref):
     flat = []
     for p in range((TI * TJ + 1) // 2):
-        pair = ref[p].astype(jnp.int32).astype(jnp.float32)
+        pair = ref[p * 16 : p * 16 + 16, :].astype(jnp.int32).astype(jnp.float32)
         flat += [pair[:8], pair[8:]]
-    factors = jnp.exp2(flat[TI * TJ]) * (1.0 / TOP)
-    return [
-        [flat[i * TJ + j] * jnp.broadcast_to(factors[:, i : i + 1], (8, 128)) for j in range(TJ)]
-        for i in range(TI)
-    ]
+    marks = jnp.broadcast_to(flat[TI * TJ][:1], (8, 128))
+    tiles = []
+    for i in range(TI):
+        top = jnp.sum(jnp.where(row_lane(i), marks, 0.0), axis=1, keepdims=True)
+        factor = jnp.exp2(jnp.broadcast_to(top, (8, 128))) * (1.0 / TOP)
+        tiles.append([flat[i * TJ + j] * factor for j in range(TJ)])
+    return tiles
 
 
 def add(a, b):
@@ -68,14 +77,22 @@
 def kernel(
     part, scales, pos, exponent, weights,
     out,
-    lev, par, sc, st, turned, bx, flag, power, held, terms, cs, xr, dr, ys, yr, zs, zq, zr, fs, fx, fy, fz,
-    load_sem, sc_sem, flag_sem, power_sem, held_sem, near, core_send, core_recv, x_send, x_recv, d_send, d_recv, y_send, y_recv, z_send, z_recv,
-    fx_send, fx_recv, fy_send, fy_recv, fz_send, fz_recv,
+    lev, par, sc, st, turned, bx, flag, power, held, terms, cs, xr, dr, ys, yr, zs, zq, zr, fs, fr,
+    load_sem, small_sem, near, scale_send, scale_recv, core_send, core_recv,
+    part_send, x_recv, early_recv, y_recv, z_send, z_recv, flag_send, flag_recv,
 ):
     inter, x = lax.axis_index("inter"), lax.axis_index("intra")
     c, zc = inter % 2, inter % ZC
     z, y = zc // 2, inter // ZC
     partner = inter + 1 - 2 * c
+
+    def load(h, side):
+        for xt in range(NX):
+            columns = pl.ds(pl.multiple_of(xt * 2 * HALF + side * HALF, 128), HALF)
+            pltpu.make_async_copy(part.at[:, :, :, columns], lev.at[h, :, xt], load_sem.at[h]).start()
+
+    load(1, 1 - c)
+    pltpu.make_async_copy(scales, sc.at[0], small_sem.at[0]).start()
 
     barrier = pltpu.get_barrier_semaphore()
 
@@ -99,23 +116,17 @@
         tell(barrier, along_y(d))
     for d in (1, NZ - 1):
         tell(barrier, along_z(d))
-    for h, side in ((1, 1 - c), (0, c)):
-        for xt in range(NX):
-            columns = pl.ds(pl.multiple_of(xt * 2 * HALF + side * HALF, 128), HALF)
-            pltpu.make_async_copy(part.at[:, :, :, columns], lev.at[h, :, xt], load_sem.at[h]).start()
-    pltpu.make_async_copy(scales, sc.at[0], sc_sem.at[0]).start()
-
-    pltpu.make_async_copy(pos, flag, flag_sem).start()
-    pltpu.make_async_copy(exponent, power, power_sem).start()
-    pltpu.make_async_copy(weights, held, held_sem).start()
-
+    load(0, c)
+    pltpu.make_async_copy(pos, flag, small_sem.at[1]).start()
+    pltpu.make_async_copy(exponent, power, small_sem.at[2]).start()
+    pltpu.make_async_copy(weights, held, small_sem.at[3]).start()
     with jax.named_scope("load"):
-        wait(sc.at[0], sc_sem.at[0])
+        wait(sc.at[0], small_sem.at[0])
         wait(lev.at[1], load_sem.at[1])
     with jax.named_scope("barrier"):
         pl.semaphore_wait(barrier, 1 + NX - 1 + 2 + 2)
     tell_both(0, along_y, NY, 1)
-    tell_both(1, along_z, NZ, 1)
+    tell_both(0, along_z, NZ, 1)
 
     def offset(q):
         return far_first(q, NY)
@@ -123,11 +134,11 @@
     def core_copy(k):
         yt = (y + offset(k)) % NY
         return pltpu.make_async_remote_copy(
-            lev.at[1, yt], par.at[yt], core_send, core_recv.at[k], (partner, x), MESH
+            lev.at[1, yt], par.at[yt], core_send, core_recv.at[(k + 3) // 4], (partner, x), MESH
         )
 
     scale_copy = pltpu.make_async_remote_copy(
-        sc.at[0], sc.at[1], sc_sem.at[1], sc_sem.at[2], (partner, x), MESH
+        sc.at[0], sc.at[1], scale_send, scale_recv, (partner, x), MESH
     )
     scale_copy.start()
 
@@ -137,11 +148,11 @@
 
     def flag_x(d):
         return pltpu.make_async_remote_copy(
-            fs.at[0], fx.at[d - 1], fx_send.at[d - 1], fx_recv.at[d - 1], (inter, (x + d) % NX), MESH
-        )
-
-    wait(flag, flag_sem)
-    wait(power, power_sem)
+            fs.at[0], fr.at[d - 1], flag_send, flag_recv.at[0], (inter, (x + d) % NX), MESH
+        )
+
+    wait(flag, small_sem.at[1])
+    wait(power, small_sem.at[2])
     fs[0] = jnp.full((1, 128), (flag[0, 0] >= 0).astype(jnp.float32), jnp.float32)
     for d in range(1, NX):
         flag_x(d).start()
@@ -175,12 +186,12 @@
 
     def x_copy(src, k, d):
         return pltpu.make_async_remote_copy(
-            src, xr.at[k, d - 1], x_send.at[k, d - 1], x_recv.at[k, d - 1], (inter, (x + d) % NX), MESH
+            src.at[:USED], xr.at[k, SIDES.index(d), :USED], part_send, x_recv.at[k], (inter, (x + d) % NX), MESH
         )
 
     def early_copy(q):
         return pltpu.make_async_remote_copy(
-            cs.at[q, 2], dr.at[q - FULL], d_send, d_recv.at[q - FULL], along_y(offset(q)), MESH
+            cs.at[q * NX + 2, :USED], dr.at[q - FULL, :USED], part_send, early_recv, along_y(offset(q)), MESH
         )
 
     def tiles_of(q, d):
@@ -191,8 +202,13 @@
 
     def produce(q):
         yt = (y + offset(q)) % NY
-        with jax.named_scope("wait_core"):
-            wait(par.at[yt], core_recv.at[q])
+        for g, (first, n) in enumerate(((0, 1), (1, 4), (5, 3))):
+
+            @pl.when(q == first)
+            def _():
+                with jax.named_scope("wait_core"):
+                    wait(par.at[:n], core_recv.at[g])
+
         tops = []
         for d in range(NX):
             xt = (x + d) % NX
@@ -211,12 +227,12 @@
                 tops.append(top_of(row))
 
         def send(d):
-            encode(tiles_of(q, d), tops[d * TI : d * TI + TI], cs.at[q, d])
+            encode(tiles_of(q, d), tops[d * TI : d * TI + TI], cs.at[q * NX + d])
 
         @pl.when(q < FULL)
         def _():
             send(2)
-            x_copy(cs.at[q, 2], q, 2).start()
+            x_copy(cs.at[q * NX + 2], q, 2).start()
 
         @pl.when(jnp.logical_and(q >= FULL, q < OWN))
         def _():
@@ -225,15 +241,14 @@
 
         for d in (1, 3):
             send(d)
-            x_copy(cs.at[q, d], q, d).start()
+            x_copy(cs.at[q * NX + d], q, d).start()
 
         @pl.when(q == FULL - 1)
         def _():
             with jax.named_scope("near0"):
-                pl.semaphore_wait(near.at[0], 2)
-                pl.semaphore_wait(near.at[1], 2)
-            tell_both(2, along_y, NY, 2)
-            tell_both(3, along_z, NZ, 2)
+                pl.semaphore_wait(near.at[0], 4)
+            tell_both(1, along_y, NY, 2)
+            tell_both(1, along_z, NZ, 2)
 
     @pl.loop(0, NY)
     def _(q):
@@ -244,18 +259,17 @@
             spread(1, 0, NY * TI)
 
     flags = fs[0]
-    for d in range(1, NX):
-        wait(fx.at[d - 1], fx_recv.at[d - 1])
-        flags = flags + fx[d - 1]
+    wait(fr.at[: NX - 1], flag_recv.at[0])
+    for n in range(NX - 1):
+        flags = flags + fr[n]
     fs[1] = flags
     with jax.named_scope("near"):
-        pl.semaphore_wait(near.at[2], 2)
-        pl.semaphore_wait(near.at[3], 2)
-    tell_both(4, along_z, NZ, 4)
+        pl.semaphore_wait(near.at[1], 4)
+    tell_both(2, along_z, NZ, 4)
 
     def flag_y(d):
         return pltpu.make_async_remote_copy(
-            fs.at[1], fy.at[d - 1], fy_send.at[d - 1], fy_recv.at[d - 1], along_y(d), MESH
+            fs.at[1], fr.at[NX + d - 2], flag_send, flag_recv.at[1], along_y(d), MESH
         )
 
     for d in range(1, NY):
@@ -263,66 +277,66 @@
 
     def y_copy(k):
         return pltpu.make_async_remote_copy(
-            ys.at[k], yr.at[k], y_send, y_recv.at[k], along_y(offset(k)), MESH
-        )
-
-    def x_sum(k, sides):
+            ys.at[k, :USED], yr.at[k, :USED], part_send, y_recv.at[jnp.maximum(k - 4, 0)], along_y(offset(k)), MESH
+        )
+
+    def x_sum(k, n):
         with jax.named_scope("wait_x"):
-            for d in sides:
-                wait(xr.at[k, d - 1], x_recv.at[k, d - 1])
+            wait(xr.at[k, :n, :USED], x_recv.at[k])
         tiles = tiles_of(k, 0)
-        for d in sides:
-            tiles = add(tiles, decode(xr.at[k, d - 1]))
+        for m in range(n):
+            tiles = add(tiles, decode(xr.at[k, m]))
         return tiles
 
     def flag_z(k):
         to = (zc + far_first(k, ZC)) % ZC
         return pltpu.make_async_remote_copy(
-            fs.at[2], fz.at[zc], fz_send, fz_recv, (y * ZC + to, x), MESH
-        )
-
-    def pass_on(k, sides):
-        tiles = x_sum(k, sides)
+            fs.at[2], fr.at[NX + NY - 2 + zc], flag_send, flag_recv.at[2], (y * ZC + to, x), MESH
+        )
+
+    def pass_on(k, n):
+        tiles = x_sum(k, n)
         encode(tiles, [top_of(row) for row in tiles], ys.at[k])
         y_copy(k).start()
 
     @pl.loop(0, FULL - 1)
     def _(k):
-        pass_on(k, (1, 3, 2))
+        pass_on(k, 3)
 
     tiles = tiles_of(OWN, 2)
+    with jax.named_scope("wait_d"):
+        wait(dr.at[:, :USED], early_recv)
     for n in range(OWN - FULL):
-        with jax.named_scope("wait_d"):
-            wait(dr.at[n], d_recv.at[n])
         tiles = add(tiles, decode(dr.at[n]))
-    encode(tiles, [top_of(row) for row in tiles], cs.at[OWN, 2])
-    x_copy(cs.at[OWN, 2], OWN, 2).start()
-
-    pass_on(FULL - 1, (1, 3, 2))
+    encode(tiles, [top_of(row) for row in tiles], cs.at[OWN * NX + 2])
+    x_copy(cs.at[OWN * NX + 2], OWN, 2).start()
+
+    pass_on(FULL - 1, 3)
 
     @pl.loop(FULL, OWN)
     def _(k):
-        pass_on(k, (1, 3))
+        pass_on(k, 2)
 
     flags = fs[1]
     with jax.named_scope("wait_fy"):
-        for d in range(1, NY):
-            wait(fy.at[d - 1], fy_recv.at[d - 1])
-            flags = flags + fy[d - 1]
+        wait(fr.at[NX - 1 : NX + NY - 2], flag_recv.at[1])
+    for n in range(NX - 1, NX + NY - 2):
+        flags = flags + fr[n]
     fs[2] = flags
-    fz[zc] = flags
+    fr[NX + NY - 2 + zc] = flags
     with jax.named_scope("near4"):
-        pl.semaphore_wait(near.at[4], 2)
+        pl.semaphore_wait(near.at[2], 2)
 
     @pl.loop(0, ZC - 1)
     def _(n):
         flag_z(n).start()
 
-    tiles = x_sum(OWN, (1, 3, 2))
-    for k in range(OWN):
+    tiles = x_sum(OWN, 3)
+    for g, (first, n) in enumerate(((0, 5), (5, 1), (6, 1))):
         with jax.named_scope("wait_y"):
-            wait(yr.at[k], y_recv.at[k])
-        tiles = add(tiles, decode(yr.at[k]))
+            wait(yr.at[first : first + n, :USED], y_recv.at[g])
+        for k in range(first, first + n):
+            tiles = add(tiles, decode(yr.at[k]))
     for i in range(TI):
         top = top_of(tiles[i])
         factor = jnp.exp2(-top) * TOP
@@ -344,38 +358,36 @@
 
     zr[zc] = zq[zc]
 
-    wait(held, held_sem)
+    wait(held, small_sem.at[3])
     for h in range(2):
         for j in range(TJ):
             at = (h * TJ + j) * 128
             out[16 + h * 8 + j : 17 + h * 8 + j, :] = held[:, at : at + 128]
 
-    for d in range(1, NX):
-        wait(fs.at[0], fx_send.at[d - 1])
-    for d in range(1, NY):
-        wait(fs.at[1], fy_send.at[d - 1])
     wait(lev.at[1], core_send)
-    for k in range(NY):
-        for d in (1, 3) if FULL <= k < OWN else (1, 2, 3):
-            wait(xr.at[k, d - 1], x_send.at[k, d - 1])
-    wait(dr, d_send)
-    wait(ys, y_send)
-    wait(fz.at[: ZC - 1], fz_send)
+    wait(cs.at[:SENT, :USED], part_send)
+    wait(fr.at[: NX + NY + ZC - 3], flag_send)
     with jax.named_scope("wait_flags"):
-        wait(fz.at[: ZC - 1], fz_recv)
-    count = functools.reduce(jnp.add, [fz[n] for n in range(ZC)])
+        wait(fr.at[NX + NY - 2 : NX + NY + ZC - 3], flag_recv.at[2])
+    count = functools.reduce(jnp.add, [fr[NX + NY - 2 + n] for n in range(ZC)])
     with jax.named_scope("wait_z"):
         wait(zr.at[: ZC - 1, : TJ + 1], z_recv)
-    wait(zr.at[: ZC - 1, : TJ + 1], z_send)
+
+    def row_sum(n, totals):
+        sums = []
+        for h in range(2):
+            codes = zr[2 * n + h].astype(jnp.int32).astype(jnp.float32)
+            factor = jnp.exp2(jnp.broadcast_to(codes[TJ : TJ + 1], (8, 128))) * (1.0 / TOP)
+            sums.append(totals[h] + codes * factor)
+        return tuple(sums)
+
+    zero = jnp.zeros((8, 128), jnp.float32)
+    totals = lax.fori_loop(0, NZ, row_sum, (zero, zero), unroll=4)
     for h in range(2):
-        total = None
-        for n in range(NZ):
-            codes = zr[2 * n + h].astype(jnp.int32).astype(jnp.float32)
-            part_sum = codes * (jnp.exp2(jnp.broadcast_to(codes[TJ : TJ + 1], (8, 128))) * (1.0 / TOP))
-            total = part_sum if total is None else total + part_sum
-        out[h * 8 : h * 8 + TJ, :] = total[:TJ]
+        out[h * 8 : h * 8 + TJ, :] = totals[h][:TJ]
     out[TJ : TJ + 1, :] = count
     out[7:8, :] = jnp.full((1, 128), power[0].astype(jnp.float32), jnp.float32)
+    wait(zr.at[: ZC - 1, : TJ + 1], z_send)
 
 
 def finish(sums, grad, block_scale, master, new_exponent, count):
@@ -406,7 +418,7 @@
         pl.BlockSpec(memory_space=m) for m in (pltpu.VMEM, pltpu.SMEM, pltpu.HBM)
     )
     f32, i16, dma = jnp.float32, jnp.int16, pltpu.SemaphoreType.DMA
-    codes = (8, 16, 128)
+    codes = (128, 128)
     sums = pl.pallas_call(
         kernel,
         out_shape=pltpu.VMEM((32, 128), f32),
@@ -423,7 +435,7 @@
             pltpu.SMEM((1,), jnp.int32),
             pltpu.VMEM((1, 2 * HALF), f32),
             pltpu.VMEM((NY, NX, TI * TJ, 8, 128), f32),
-            pltpu.VMEM((NY, NX, *codes), i16),
+            pltpu.VMEM((NY * NX, *codes), i16),
             pltpu.VMEM((NY, NX - 1, *codes), i16),
             pltpu.VMEM((OWN - FULL, *codes), i16),
             pltpu.VMEM((OWN, *codes), i16),
@@ -432,12 +444,9 @@
             pltpu.VMEM((ZC, 8, 128), i16),
             pltpu.VMEM((ZC, 8, 128), i16),
             pltpu.VMEM((3, 1, 128), f32),
-            pltpu.VMEM((NX - 1, 1, 128), f32),
-            pltpu.VMEM((NY - 1, 1, 128), f32),
-            pltpu.VMEM((ZC, 1, 128), f32),
-            dma((2,)), dma((3,)), dma, dma, dma, pltpu.SemaphoreType.REGULAR((5,)), dma, dma((NY,)), dma((NY, NX - 1)), dma((NY, NX - 1)),
-            dma, dma((OWN - FULL,)), dma, dma((OWN,)), dma, dma,
-            dma((NX - 1,)), dma((NX - 1,)), dma((NY - 1,)), dma((NY - 1,)), dma, dma,
+            pltpu.VMEM((NX + NY - 2 + ZC, 1, 128), f32),
+            dma((2,)), dma((4,)), pltpu.SemaphoreType.REGULAR((3,)), dma, dma, dma, dma((3,)),
+            dma, dma((NY,)), dma, dma((3,)), dma, dma, dma, dma((3,)),
         ],
         compiler_params=pltpu.CompilerParams(collective_id=0, has_side_effects=True),
         name="exchange",

time: 41.1 us -> 40.3 us (0.981)
  Pallas kernels: 39 us -> 38.2 us
    pallas_call x1, Pallas kernels: 38.2 us -> 37.4 us  [on_device(): pl.pallas_call(kernel, out_shape=pltpu.VMEM((32, 128), f32), in_specs=[hb...]
where the time goes in v5:
time: 40.3 us; the launch traced here: 40.1 us
  Pallas kernels  38.2 us (95%)
  between operations  1.93 us (5%)
    pallas_call x1, Pallas kernels, on_device(): pl.pallas_call(kernel, out_shape=pltpu.VMEM((32, 128), f32), in_specs=[hb...  37.4 us

profile of v5, /device:TPU:1, one launch (start us, length us, event | category | flops | bytes accessed | tf_op | source)
XLA Modules:
  0.0 40.1 jit_solution(12190241436130423861)
XLA Ops:
  1.9 37.4 %exchange.1.sums = f32[32,128]{1,0:T(8,128)S(1)} custom-call(bf16[8,3,8,5120]{3,2,1,0:T(8,128)(2,1)} %bitcast.8, bf16[20,192]{1,0:T(8,128)(2,1)} %bitcast.9, s32[1,1]{1,0:T(1,128)S(6)} %copy.10.pos, s32[1]{0:T(128)} %bitcast.7.exponent, f32[1,1280]{1,0:T(1,128)} %weights.1), custom_call_target="tpu_custom_call" | custom-call | tf_op jit(solution)/shard_map/exchange/pallas_call | solution.py:422
  39.3 0.8 %finish.1 = (f32[1,1280]{1,0:T(1,128)}, f32[1,5]{1,0:T(1,128)}, f32[1,1280]{1,0:T(1,128)}, s32[1]{0:T(128)}, s32[1]{0:T(128)}) custom-call(f32[32,128]{1,0:T(8,128)S(1)} %exchange.1.sums), custom_call_target="tpu_custom_call" | custom-call | tf_op jit(solution)/shard_map/finish/pallas_call | solution.py:460

commit v6 on v5

--- a/solution.py
+++ b/solution.py
@@ -77,7 +77,7 @@
 def kernel(
     part, scales, pos, exponent, weights,
     out,
-    lev, par, sc, st, turned, bx, flag, power, held, terms, cs, xr, dr, ys, yr, zs, zq, zr, fs, fr,
+    lev, head, par, sc, st, turned, bx, flag, power, held, terms, cs, xr, dr, ys, yr, zs, zq, zr, fs, fr,
     load_sem, small_sem, near, scale_send, scale_recv, core_send, core_recv,
     part_send, x_recv, early_recv, y_recv, z_send, z_recv, flag_send, flag_recv,
 ):
@@ -86,15 +86,25 @@
     z, y = zc // 2, inter // ZC
     partner = inter + 1 - 2 * c
 
+    def offset(q):
+        return far_first(q, NY)
+
+    def columns(xt, side):
+        return pl.ds(pl.multiple_of(xt * 2 * HALF + side * HALF, 128), HALF)
+
     def load(h, side):
         for xt in range(NX):
-            columns = pl.ds(pl.multiple_of(xt * 2 * HALF + side * HALF, 128), HALF)
-            pltpu.make_async_copy(part.at[:, :, :, columns], lev.at[h, :, xt], load_sem.at[h]).start()
-
-    load(1, 1 - c)
+            pltpu.make_async_copy(part.at[:, :, :, columns(xt, side)], lev.at[h, :, xt], load_sem.at[h]).start()
+
+    first_y = (y + offset(0)) % NY
+    for xt in range(NX):
+        pltpu.make_async_copy(part.at[first_y, :, :, columns(xt, 1 - c)], head.at[xt], load_sem.at[2]).start()
     pltpu.make_async_copy(scales, sc.at[0], small_sem.at[0]).start()
 
     barrier = pltpu.get_barrier_semaphore()
+
+    def along_x(d):
+        return (inter, (x + d) % NX)
 
     def along_y(d):
         return ((y + d) % NY * ZC + zc, x)
@@ -110,52 +120,51 @@
         tell(near.at[sem], along(n - d))
 
     tell(barrier, (partner, x))
-    for d in range(1, NX):
-        tell(barrier, (inter, (x + d) % NX))
+    for d in (1, NX - 1):
+        tell(barrier, along_x(d))
     for d in (1, NY - 1):
         tell(barrier, along_y(d))
     for d in (1, NZ - 1):
         tell(barrier, along_z(d))
+    load(1, 1 - c)
     load(0, c)
     pltpu.make_async_copy(pos, flag, small_sem.at[1]).start()
     pltpu.make_async_copy(exponent, power, small_sem.at[2]).start()
     pltpu.make_async_copy(weights, held, small_sem.at[3]).start()
-    with jax.named_scope("load"):
-        wait(sc.at[0], small_sem.at[0])
-        wait(lev.at[1], load_sem.at[1])
     with jax.named_scope("barrier"):
-        pl.semaphore_wait(barrier, 1 + NX - 1 + 2 + 2)
+        pl.semaphore_wait(barrier, 1 + 2 + 2 + 2)
+    tell_both(3, along_x, NX, 1)
     tell_both(0, along_y, NY, 1)
     tell_both(0, along_z, NZ, 1)
 
-    def offset(q):
-        return far_first(q, NY)
-
-    def core_copy(k):
+    def core_copy(k, source):
         yt = (y + offset(k)) % NY
         return pltpu.make_async_remote_copy(
-            lev.at[1, yt], par.at[yt], core_send, core_recv.at[(k + 3) // 4], (partner, x), MESH
+            source, par.at[yt], core_send, core_recv.at[(k + 3) // 4], (partner, x), MESH
         )
 
     scale_copy = pltpu.make_async_remote_copy(
         sc.at[0], sc.at[1], scale_send, scale_recv, (partner, x), MESH
     )
-    scale_copy.start()
-
-    @pl.loop(0, NY)
+    with jax.named_scope("load"):
+        wait(sc.at[0], small_sem.at[0])
+        scale_copy.start()
+        wait(head, load_sem.at[2])
+        core_copy(0, head).start()
+        wait(lev.at[1], load_sem.at[1])
+
+    @pl.loop(1, NY)
     def _(k):
-        core_copy(k).start()
+        core_copy(k, lev.at[1, (y + offset(k)) % NY]).start()
 
     def flag_x(d):
         return pltpu.make_async_remote_copy(
-            fs.at[0], fr.at[d - 1], flag_send, flag_recv.at[0], (inter, (x + d) % NX), MESH
+            fs.at[0], fr.at[d - 1], flag_send, flag_recv.at[0], along_x(d), MESH
         )
 
     wait(flag, small_sem.at[1])
     wait(power, small_sem.at[2])
     fs[0] = jnp.full((1, 128), (flag[0, 0] >= 0).astype(jnp.float32), jnp.float32)
-    for d in range(1, NX):
-        flag_x(d).start()
 
     def turn(h):
         st[:20, : NY * ZC] = sc[h].astype(jnp.float32)
@@ -186,7 +195,7 @@
 
     def x_copy(src, k, d):
         return pltpu.make_async_remote_copy(
-            src.at[:USED], xr.at[k, SIDES.index(d), :USED], part_send, x_recv.at[k], (inter, (x + d) % NX), MESH
+            src.at[:USED], xr.at[k, SIDES.index(d), :USED], part_send, x_recv.at[k], along_x(d), MESH
         )
 
     def early_copy(q):
@@ -197,6 +206,10 @@
     def tiles_of(q, d):
         return [[terms[q, d, i * TJ + j] for j in range(TJ)] for i in range(TI)]
 
+    with jax.named_scope("near_x"):
+        pl.semaphore_wait(near.at[3], 2)
+    for d in range(1, NX):
+        flag_x(d).start()
     with jax.named_scope("spread1"):
         spread(1, (y + offset(0)) % NY * TI, TI)
 
@@ -426,6 +439,7 @@
         out_specs=vmem,
         scratch_shapes=[
             pltpu.VMEM((2, NY, NX, TI, 8, HALF), jnp.bfloat16),
+            pltpu.VMEM((NX, TI, 8, HALF), jnp.bfloat16),
             pltpu.VMEM((NY, NX, TI, 8, HALF), jnp.bfloat16),
             pltpu.VMEM((2, 20, NY * ZC), jnp.bfloat16),
             pltpu.VMEM((32, 256), f32),
@@ -445,7 +459,7 @@
             pltpu.VMEM((ZC, 8, 128), i16),
             pltpu.VMEM((3, 1, 128), f32),
             pltpu.VMEM((NX + NY - 2 + ZC, 1, 128), f32),
-            dma((2,)), dma((4,)), pltpu.SemaphoreType.REGULAR((3,)), dma, dma, dma, dma((3,)),
+            dma((3,)), dma((4,)), pltpu.SemaphoreType.REGULAR((4,)), dma, dma, dma, dma((3,)),
             dma, dma((NY,)), dma, dma((3,)), dma, dma, dma, dma((3,)),
         ],
         compiler_params=pltpu.CompilerParams(collective_id=0, has_side_effects=True),

time: 40.3 us -> 40.1 us (level)
  no operation moved by 1% of the time
where the time goes in v6:
time: 40.1 us; the launch traced here: 40 us
  Pallas kernels  38 us (95%)
  between operations  1.93 us (5%)
    pallas_call x1, Pallas kernels, on_device(): pl.pallas_call(kernel, out_shape=pltpu.VMEM((32, 128), f32), in_specs=[hb...  37.2 us

profile of v6, /device:TPU:1, one launch (start us, length us, event | category | flops | bytes accessed | tf_op | source)
XLA Modules:
  0.0 40.0 jit_solution(15374951875333772365)
XLA Ops:
  1.9 37.2 %exchange.1.sums = f32[32,128]{1,0:T(8,128)S(1)} custom-call(bf16[8,3,8,5120]{3,2,1,0:T(8,128)(2,1)} %bitcast.8, bf16[20,192]{1,0:T(8,128)(2,1)} %bitcast.9, s32[1,1]{1,0:T(1,128)S(6)} %copy.10.pos, s32[1]{0:T(128)} %bitcast.7.exponent, f32[1,1280]{1,0:T(1,128)} %weights.1), custom_call_target="tpu_custom_call" | custom-call | tf_op jit(solution)/shard_map/exchange/pallas_call | solution.py:435
  39.2 0.8 %finish.1 = (f32[1,1280]{1,0:T(1,128)}, f32[1,5]{1,0:T(1,128)}, f32[1,1280]{1,0:T(1,128)}, s32[1]{0:T(128)}, s32[1]{0:T(128)}) custom-call(f32[32,128]{1,0:T(8,128)S(1)} %exchange.1.sums), custom_call_target="tpu_custom_call" | custom-call | tf_op jit(solution)/shard_map/finish/pallas_call | solution.py:474

commit v7 on v6

--- a/solution.py
+++ b/solution.py
@@ -94,11 +94,11 @@
 
     def load(h, side):
         for xt in range(NX):
-            pltpu.make_async_copy(part.at[:, :, :, columns(xt, side)], lev.at[h, :, xt], load_sem.at[h]).start()
+            pltpu.make_async_copy(part.at[:, :, :, columns(xt, side)], lev.at[side, :, xt], load_sem.at[h]).start()
 
     first_y = (y + offset(0)) % NY
     for xt in range(NX):
-        pltpu.make_async_copy(part.at[first_y, :, :, columns(xt, 1 - c)], head.at[xt], load_sem.at[2]).start()
+        pltpu.make_async_copy(part.at[first_y, :, :, columns(xt, c)], head.at[xt], load_sem.at[2]).start()
     pltpu.make_async_copy(scales, sc.at[0], small_sem.at[0]).start()
 
     barrier = pltpu.get_barrier_semaphore()
@@ -108,6 +108,9 @@
 
     def along_y(d):
         return ((y + d) % NY * ZC + zc, x)
+
+    def across_y(d):
+        return ((y + d) % NY * ZC + zc + 1 - 2 * c, x)
 
     def along_z(d):
         return (y * ZC + (zc + 2 * d) % ZC, x)
@@ -124,15 +127,16 @@
         tell(barrier, along_x(d))
     for d in (1, NY - 1):
         tell(barrier, along_y(d))
+        tell(barrier, across_y(d))
     for d in (1, NZ - 1):
         tell(barrier, along_z(d))
-    load(1, 1 - c)
-    load(0, c)
+    load(1, c)
+    load(0, 1 - c)
     pltpu.make_async_copy(pos, flag, small_sem.at[1]).start()
     pltpu.make_async_copy(exponent, power, small_sem.at[2]).start()
     pltpu.make_async_copy(weights, held, small_sem.at[3]).start()
     with jax.named_scope("barrier"):
-        pl.semaphore_wait(barrier, 1 + 2 + 2 + 2)
+        pl.semaphore_wait(barrier, 1 + 2 + 4 + 2)
     tell_both(3, along_x, NX, 1)
     tell_both(0, along_y, NY, 1)
     tell_both(0, along_z, NZ, 1)
@@ -151,11 +155,12 @@
         scale_copy.start()
         wait(head, load_sem.at[2])
         core_copy(0, head).start()
-        wait(lev.at[1], load_sem.at[1])
+        wait(lev.at[c], load_sem.at[1])
+        wait(lev.at[1 - c], load_sem.at[0])
 
     @pl.loop(1, NY)
     def _(k):
-        core_copy(k, lev.at[1, (y + offset(k)) % NY]).start()
+        core_copy(k, lev.at[jnp.where(k == OWN, 1 - c, c), (y + offset(k)) % NY]).start()
 
     def flag_x(d):
         return pltpu.make_async_remote_copy(
@@ -172,11 +177,11 @@
 
     block = lax.broadcasted_iota(jnp.int32, (32, 128), 0)
 
-    def spread(h, first, n):
+    def spread(h, first, n, side):
         rows = turned[h, pl.ds(pl.multiple_of(first * 8, 8), n * 8), :].astype(jnp.bfloat16)
         for t in range(0, NB * NX, 2):
             picks = [
-                jnp.where(block == u // NB * TJ + 2 * c + u % NB, 1.0, 0.0).astype(jnp.bfloat16)
+                jnp.where(block == u // NB * TJ + 2 * side + u % NB, 1.0, 0.0).astype(jnp.bfloat16)
                 for u in (t, t + 1)
             ]
             both = jnp.dot(rows, jnp.concatenate(picks, axis=1), preferred_element_type=jnp.float32)
@@ -186,9 +191,9 @@
     st[...] = jnp.zeros((32, 256), jnp.float32)
     with jax.named_scope("spread0"):
         turn(0)
-        spread(0, 0, NY * TI)
+        spread(0, 0, NY * TI, 1 - c)
+        spread(0, y * TI, TI, c)
     with jax.named_scope("wait_scale"):
-        wait(lev.at[0], load_sem.at[0])
         scale_copy.wait()
     with jax.named_scope("turn"):
         turn(1)
@@ -200,7 +205,7 @@
 
     def early_copy(q):
         return pltpu.make_async_remote_copy(
-            cs.at[q * NX + 2, :USED], dr.at[q - FULL, :USED], part_send, early_recv, along_y(offset(q)), MESH
+            cs.at[q * NX + 2, :USED], dr.at[q - FULL, :USED], part_send, early_recv, across_y(offset(q)), MESH
         )
 
     def tiles_of(q, d):
@@ -211,7 +216,7 @@
     for d in range(1, NX):
         flag_x(d).start()
     with jax.named_scope("spread1"):
-        spread(1, (y + offset(0)) % NY * TI, TI)
+        spread(1, (y + offset(0)) % NY * TI, TI, 1 - c)
 
     def produce(q):
         yt = (y + offset(q)) % NY
@@ -222,6 +227,8 @@
                 with jax.named_scope("wait_core"):
                     wait(par.at[:n], core_recv.at[g])
 
+        side = jnp.where(q == OWN, c, 1 - c)
+        even = side == 0
         tops = []
         for d in range(NX):
             xt = (x + d) % NX
@@ -229,9 +236,8 @@
                 row = None
                 for h in range(2):
                     b = [bx[h, yt * TI + i, xt * NB + n] for n in range(NB)]
-                    even = c == 0
                     b = [b[0], jnp.where(even, b[0], b[1]), b[1], jnp.where(even, b[1], b[2]), b[2]]
-                    levels = lev[0, yt, xt, i] if h == 0 else par[yt, xt, i]
+                    levels = par[yt, xt, i] if h else lev[side, yt, xt, i]
                     levels = levels.astype(jnp.float32)
                     term = [levels[:, j * 128 : (j + 1) * 128] * b[j] for j in range(TJ)]
                     row = term if row is None else [p + q for p, q in zip(row, term)]
@@ -269,7 +275,8 @@
 
         @pl.when(q == 0)
         def _():
-            spread(1, 0, NY * TI)
+            spread(1, 0, NY * TI, 1 - c)
+            spread(1, y * TI, TI, c)
 
     flags = fs[0]
     wait(fr.at[: NX - 1], flag_recv.at[0])
@@ -282,7 +289,7 @@
 
     def flag_y(d):
         return pltpu.make_async_remote_copy(
-            fs.at[1], fr.at[NX + d - 2], flag_send, flag_recv.at[1], along_y(d), MESH
+            fs.at[1], fr.at[NX + d - 2], flag_send, flag_recv.at[1], across_y(d), MESH
         )
 
     for d in range(1, NY):
@@ -290,7 +297,7 @@
 
     def y_copy(k):
         return pltpu.make_async_remote_copy(
-            ys.at[k, :USED], yr.at[k, :USED], part_send, y_recv.at[jnp.maximum(k - 4, 0)], along_y(offset(k)), MESH
+            ys.at[k, :USED], yr.at[k, :USED], part_send, y_recv.at[jnp.maximum(k - 4, 0)], across_y(offset(k)), MESH
         )
 
     def x_sum(k, n):

time: 40.1 us -> 39.9 us (level)
  no operation moved by 1% of the time
where the time goes in v7:
time: 39.9 us; the launch traced here: 39.7 us
  Pallas kernels  37.8 us (95%)
  between operations  1.93 us (5%)
    pallas_call x1, Pallas kernels, on_device(): pl.pallas_call(kernel, out_shape=pltpu.VMEM((32, 128), f32), in_specs=[hb...  37 us

profile of v7, /device:TPU:1, one launch (start us, length us, event | category | flops | bytes accessed | tf_op | source)
XLA Modules:
  0.0 39.7 jit_solution(6999266293995483366)
XLA Ops:
  1.9 37.0 %exchange.1.sums = f32[32,128]{1,0:T(8,128)S(1)} custom-call(bf16[8,3,8,5120]{3,2,1,0:T(8,128)(2,1)} %bitcast.8, bf16[20,192]{1,0:T(8,128)(2,1)} %bitcast.9, s32[1,1]{1,0:T(1,128)S(6)} %copy.10.pos, s32[1]{0:T(128)} %bitcast.7.exponent, f32[1,1280]{1,0:T(1,128)} %weights.1), custom_call_target="tpu_custom_call" | custom-call | tf_op jit(solution)/shard_map/exchange/pallas_call | solution.py:442
  38.9 0.8 %finish.1 = (f32[1,1280]{1,0:T(1,128)}, f32[1,5]{1,0:T(1,128)}, f32[1,1280]{1,0:T(1,128)}, s32[1]{0:T(128)}, s32[1]{0:T(128)}) custom-call(f32[32,128]{1,0:T(8,128)S(1)} %exchange.1.sums), custom_call_target="tpu_custom_call" | custom-call | tf_op jit(solution)/shard_map/finish/pallas_call | solution.py:481

commit v8 on v7

--- a/solution.py
+++ b/solution.py
@@ -211,10 +211,6 @@
     def tiles_of(q, d):
         return [[terms[q, d, i * TJ + j] for j in range(TJ)] for i in range(TI)]
 
-    with jax.named_scope("near_x"):
-        pl.semaphore_wait(near.at[3], 2)
-    for d in range(1, NX):
-        flag_x(d).start()
     with jax.named_scope("spread1"):
         spread(1, (y + offset(0)) % NY * TI, TI, 1 - c)
 
@@ -251,6 +247,14 @@
         @pl.when(q < FULL)
         def _():
             send(2)
+
+            @pl.when(q == 0)
+            def _():
+                with jax.named_scope("near_x"):
+                    pl.semaphore_wait(near.at[3], 2)
+                for d in range(1, NX):
+                    flag_x(d).start()
+
             x_copy(cs.at[q * NX + 2], q, 2).start()
 
         @pl.when(jnp.logical_and(q >= FULL, q < OWN))

time: 39.9 us -> 40 us (level)
  no operation moved by 1% of the time
where the time goes in v8:
time: 40 us; the launch traced here: 39.8 us
  Pallas kernels  37.9 us (95%)
  between operations  1.93 us (5%)
    pallas_call x1, Pallas kernels, on_device(): pl.pallas_call(kernel, out_shape=pltpu.VMEM((32, 128), f32), in_specs=[hb...  37.1 us

profile of v8, /device:TPU:1, one launch (start us, length us, event | category | flops | bytes accessed | tf_op | source)
XLA Modules:
  0.0 39.8 jit_solution(6283670760324568409)
XLA Ops:
  1.9 37.1 %exchange.1.sums = f32[32,128]{1,0:T(8,128)S(1)} custom-call(bf16[8,3,8,5120]{3,2,1,0:T(8,128)(2,1)} %bitcast.8, bf16[20,192]{1,0:T(8,128)(2,1)} %bitcast.9, s32[1,1]{1,0:T(1,128)S(6)} %copy.10.pos, s32[1]{0:T(128)} %bitcast.7.exponent, f32[1,1280]{1,0:T(1,128)} %weights.1), custom_call_target="tpu_custom_call" | custom-call | tf_op jit(solution)/shard_map/exchange/pallas_call | solution.py:446
  39.0 0.8 %finish.1 = (f32[1,1280]{1,0:T(1,128)}, f32[1,5]{1,0:T(1,128)}, f32[1,1280]{1,0:T(1,128)}, s32[1]{0:T(128)}, s32[1]{0:T(128)}) custom-call(f32[32,128]{1,0:T(8,128)S(1)} %exchange.1.sums), custom_call_target="tpu_custom_call" | custom-call | tf_op jit(solution)/shard_map/finish/pallas_call | solution.py:485
